TPU v7x, 512 devices: a whole 4x8x8 slice. The times are simulated.
512 devices in a mesh: shear: 64 (over z_hi, y, x), cross: 8 (over z_lo, core).
Axes of the slice: x: 4, y: 8, z: 8 (z_hi: 2, z_lo: 4; z = z_hi * 4 + z_lo), core: 2. Of those that a mesh axis runs over, the one named last changes fastest.
Arguments:
- positions: float32 [3, 64, 16, 8, 256], P(None, 'shear', None, 'cross'), may hold values from 0 to 1
- masses: float32 [64, 16, 8, 256], P('shear', None, 'cross'), may hold values from 0.002 to 0.008
- counts: int32 [64, 16, 8], P('shear', None, 'cross'), may hold values from 32 to 256
- shear_offset: int32 [1], replicated, may hold values from 0 to 15
Outputs:
- density: float32 [64, 16, 8, 256], P('shear', None, 'cross')
Inputs may be any that keep to these rules, and one draw needn't show every extreme that they name: `shear_offset`: a whole number of cells.
All inputs are finite; a program needn't handle non-finite values.
Results may differ from a plain program's by a relative error of at most 0.0003.
Values sent between devices are 32-bit elements; how exact they have to be, the bound alone decides.
No kernel may reach another device: no remote copies, remote signals or barrier semaphores. Data moves between devices by JAX's collectives and lax.ppermute only.
A program may use at most 64 MiB of HBM per device.

v0:
```python
import jax
import jax.numpy as jnp
from jax import lax
from jax.sharding import PartitionSpec as P


def extended_2(block, sides, width):
    for axis, dim in sides:
        count = lax.axis_size(axis)
        forward = [(i, i + 1) for i in range(count - 1)]
        forward.append((count - 1, 0))
        backward = [(target, source) for source, target in forward]
        low = lax.ppermute(
            lax.slice_in_dim(block, block.shape[dim] - width, None, axis=dim), axis, forward
        )
        high = lax.ppermute(lax.slice_in_dim(block, 0, width, axis=dim), axis, backward)
        block = jnp.concatenate([low, block, high], axis=dim)
    return block


def shifted(block, axis, distance):
    devices = range(lax.axis_size(axis))
    route = [((i - distance) % len(devices), i) for i in devices]
    return lax.ppermute(block, axis, route)


def spline(squared):
    radius = jnp.sqrt(squared) * 4.0
    inner_part = 1.0 - 1.5 * radius * radius + 0.75 * radius * radius * radius
    outer_part = 0.25 * jnp.maximum(2.0 - radius, 0.0) ** 3
    return jnp.where(radius < 1.0, inner_part, outer_part) * (64.0 / 3.141592653589793)


def distance_sq(target, source_pos, offset_vec):
    squared = None
    for component in range(3):
        moved = source_pos[component] + offset_vec[component]
        gap = target[component][..., :, None] - moved[..., None, :]
        squared = gap * gap if squared is None else squared + gap * gap
    return squared


def shards(positions, masses, counts, shear_offset):
    slot_index = lax.broadcasted_iota(jnp.int32, masses.shape, 3)
    is_valid = slot_index < counts[..., None]
    weight = jnp.where(is_valid, masses, jnp.float32(0.0))
    particle_data = jnp.concatenate([positions, weight[None]], 0)
    offset = shear_offset[0]
    shear_index = lax.axis_index("shear")
    cycle_size = lax.axis_size("shear")
    cells_y = masses.shape[0]
    cells_z = masses.shape[2]
    padded = extended_2(particle_data, (("shear", 1), ("cross", 3)), 1)
    lower_row = padded[:, :1]
    upper_row = padded[:, -1:]
    lower_row = jnp.where(shear_index == 0, jnp.roll(lower_row, offset, axis=2), lower_row)
    upper_row = jnp.where(
        shear_index == cycle_size - 1, jnp.roll(upper_row, -offset, axis=2), upper_row
    )
    extended = jnp.concatenate([lower_row, padded[:, 1:-1], upper_row], 1)
    target = extended[:3, 1 : 1 + cells_y, :, 1 : 1 + cells_z]
    target_mass = extended[3, 1 : 1 + cells_y, :, 1 : 1 + cells_z]

    def source(step_y, step_z, step_x):
        picked = extended[
            :, 1 + step_y : 1 + step_y + cells_y, :, 1 + step_z : 1 + step_z + cells_z
        ]
        return jnp.roll(picked, -step_x, axis=2)

    density = jnp.zeros(masses.shape, jnp.float32)
    returned = jnp.zeros((cells_y + 2, masses.shape[1], cells_z + 2, masses.shape[3]), jnp.float32)
    half_steps = [
        (step_y, step_z, step_x)
        for step_y in (0, 1)
        for step_z in (-1, 0, 1)
        for step_x in (-1, 0, 1)
        if (step_y, step_z, step_x) >= (0, 0, 0)
    ]
    for step_y, step_z, step_x in half_steps:
        source_cells = source(step_y, step_z, step_x)
        offset_vec = (float(step_y), float(step_x), float(step_z))
        kernel = spline(distance_sq(target, source_cells[:3], offset_vec))
        density = density + jnp.sum(kernel * source_cells[3][..., None, :], axis=-1)
        if (step_y, step_z, step_x) != (0, 0, 0):
            reflected = jnp.sum(kernel * target_mass[..., :, None], axis=-2)
            reflected = jnp.roll(reflected, step_x, axis=1)
            returned = returned.at[
                1 + step_y : 1 + step_y + cells_y, :, 1 + step_z : 1 + step_z + cells_z
            ].add(reflected)
    from_below = shifted(returned[:, :, cells_z + 1], "cross", 1)
    from_above = shifted(returned[:, :, 0], "cross", -1)
    returned = returned.at[:, :, 1].add(from_below)
    returned = returned.at[:, :, cells_z].add(from_above)
    top_row = returned[cells_y + 1, :, 1 : 1 + cells_z]
    arrived = shifted(top_row, "shear", 1)
    arrived = jnp.where(shear_index == 0, jnp.roll(arrived, offset, axis=0), arrived)
    owned = returned[1 : 1 + cells_y, :, 1 : 1 + cells_z].at[0].add(arrived)
    density = density + owned
    return jnp.where(is_valid, density, jnp.float32(0.0))


def solution(mesh):
    in_specs = (
        P(None, "shear", None, "cross", None),
        P("shear", None, "cross", None),
        P("shear", None, "cross"),
        P(),
    )
    out_specs = P("shear", None, "cross", None)
    return jax.shard_map(shards, mesh=mesh, in_specs=in_specs, out_specs=out_specs, check_vma=False)
```

profile of v0, /device:TPU:1, one launch (start us, length us, event | category | flops | bytes accessed | tf_op | source)
XLA Modules:
  0.0 143.5 jit_solution(123626709004466542)
XLA Ops:
  0.0 0.8 constant_dynamic-update-slice_fusion
  0.8 0.8 multiply_bitcast_fusion
  1.6 16.6 %collective-permute-start.1 = (f32[4,1,16,1,256]{4,3,2,1,0:T(1,128)S(1)}, f32[4,1,16,1,256]{4,3,2,1,0:T(1,128)S(1)}, u32[]{:S(2)}, u32[]{:S(2)}) collective-permute-start(f32[4,1,16,1,256]{4,3,2,1,0:T(1,128)S(1)} %copy_dynamic-update-slice_fusion), channel_id=1, source_target_pairs={{8,0},{16,8},{24,16},{32,24},{40,32},{48,40},{56,48},{64,56},{72,6... | collective-permute-start | bytes 196616 | tf_op jit(solution)/shard_map/ppermute | solution.py:16
  18.2 1.9 %collective-permute-start = (f32[4,1,16,1,256]{4,3,2,1,0:T(1,128)S(1)}, f32[4,1,16,1,256]{4,3,2,1,0:T(1,128)S(1)}, u32[]{:S(2)}, u32[]{:S(2)}) collective-permute-start(f32[4,1,16,1,256]{4,3,2,1,0:T(1,128)S(1)} %copy_dynamic-update-slice_fusion), channel_id=1, source_target_pairs={{0,8},{8,16},{16,24},{24,32},{32,40},{40,48},{48,56},{56,64},{64,7... | collective-permute-start | bytes 196616 | tf_op jit(solution)/shard_map/ppermute | solution.py:13
  20.1 0.8 fusion.127
  20.9 0.1 fusion.92
  21.7 0.0 collective-permute-done.1
  21.7 10.3 %collective-permute-done = f32[4,1,16,1,256]{4,3,2,1,0:T(1,128)S(1)} collective-permute-done((f32[4,1,16,1,256]{4,3,2,1,0:T(1,128)S(1)}, f32[4,1,16,1,256]{4,3,2,1,0:T(1,128)S(1)}, u32[]{:S(2)}, u32[]{:S(2)}) %collective-permute-start) | collective-permute-done | bytes 65568 | tf_op jit(solution)/shard_map/ppermute | solution.py:13
  32.0 0.2 pad_maximum_fusion.4
  32.2 5.3 %collective-permute-start.3 = (f32[4,3,16,1,256]{4,3,2,1,0:T(1,128)S(1)}, f32[4,3,16,1,256]{4,3,2,1,0:T(1,128)S(1)}, u32[]{:S(2)}, u32[]{:S(2)}) collective-permute-start(f32[4,3,16,1,256]{4,3,2,1,0:T(1,128)S(1)} %pad_maximum_fusion.4), channel_id=1, source_target_pairs={{0,1},{1,2},{2,3},{3,4},{4,5},{5,6},{6,7},{7,0},{8,9},{9,10},{10,1... | collective-permute-start | bytes 589832 | tf_op jit(solution)/shard_map/ppermute | solution.py:13
  37.6 1.9 %collective-permute-start.2 = (f32[4,3,16,1,256]{4,3,2,1,0:T(1,128)S(1)}, f32[4,3,16,1,256]{4,3,2,1,0:T(1,128)S(1)}, u32[]{:S(2)}, u32[]{:S(2)}) collective-permute-start(f32[4,3,16,1,256]{4,3,2,1,0:T(1,128)S(1)} %pad_maximum_fusion.4), channel_id=1, source_target_pairs={{1,0},{2,1},{3,2},{4,3},{5,4},{6,5},{7,6},{0,7},{9,8},{10,9},{11,1... | collective-permute-start | bytes 589832 | tf_op jit(solution)/shard_map/ppermute | solution.py:16
  39.5 0.7 collective-permute-done.3
  40.2 4.4 %collective-permute-done.2 = f32[4,3,16,1,256]{4,3,2,1,0:T(1,128)S(1)} collective-permute-done((f32[4,3,16,1,256]{4,3,2,1,0:T(1,128)S(1)}, f32[4,3,16,1,256]{4,3,2,1,0:T(1,128)S(1)}, u32[]{:S(2)}, u32[]{:S(2)}) %collective-permute-start.2) | collective-permute-done | bytes 196640 | tf_op jit(solution)/shard_map/ppermute | solution.py:16
  44.6 0.2 pad_maximum_fusion
  44.7 0.2 fusion.45
  45.0 0.2 slice_add_fusion.6
  45.2 0.2 fusion.123
  45.4 0.1 fusion.125
  45.5 0.1 fusion.90
  45.7 0.1 fusion.113
  45.9 20.8 %multiply_reduce_fusion.13 = (f32[16,256]{1,0:T(8,128)S(1)}, f32[16,256]{1,0:T(8,128)S(1)}, f32[16,256]{1,0:T(8,128)S(1)}, f32[16,256]{1,0:T(8,128)S(1)}, f32[16...) fusion(f32[16,256]{1,0:T(8,128)S(1)} %bitcast.261, f32[16,256]{1,0:T(8,128)S(1)} %bitcast.258, ...), kind=kLoop, calls=%fused_computation.85 | loop fusion | flops 111120384 | bytes 376832 | tf_op jit(solution)/shard_map/reduce_sum | solution.py:83
  66.7 0.1 fusion.89
  66.9 16.2 %multiply_reduce_fusion.15 = (f32[16,256]{1,0:T(8,128)S(1)}, f32[16,256]{1,0:T(8,128)S(1)}, f32[16,256]{1,0:T(8,128)S(1)}, f32[16,256]{1,0:T(8,128)S(1)}, f32[16,256]{1,0:T(8,128)S(1)}, /*index=5*/f32[16,256]{1,0:T(8,128)S(1)}) fusion(f32[16,256]{1,0:T(8,128)S(1)} %bitcast.240, f32[16,256]{1,0:T(8,128)S(1)} %bitcast.244, ...), kind=kLoop, calls=%fused_computation.89 | loop fusion | flops 84910080 | bytes 360448 | tf_op jit(solution)/shard_map/reduce_sum | solution.py:83
  83.2 0.1 fusion.87
  83.5 16.2 %multiply_reduce_fusion.16 = (f32[16,256]{1,0:T(8,128)S(1)}, f32[16,256]{1,0:T(8,128)S(1)}, f32[16,256]{1,0:T(8,128)S(1)}, f32[16,256]{1,0:T(8,128)S(1)}, f32[16,256]{1,0:T(8,128)S(1)}, /*index=5*/f32[16,256]{1,0:T(8,128)S(1)}) fusion(f32[16,256]{1,0:T(8,128)S(1)} %bitcast.267, f32[16,256]{1,0:T(8,128)S(1)} %bitcast.266, ...), kind=kLoop, calls=%fused_computation.91 | loop fusion | flops 84910080 | bytes 360448 | tf_op jit(solution)/shard_map/reduce_sum | solution.py:83
  99.9 16.2 %multiply_reduce_fusion.14 = (f32[16,256]{1,0:T(8,128)S(1)}, f32[16,256]{1,0:T(8,128)S(1)}, f32[16,256]{1,0:T(8,128)S(1)}, f32[16,256]{1,0:T(8,128)S(1)}, f32[16,256]{1,0:T(8,128)S(1)}, /*index=5*/f32[16,256]{1,0:T(8,128)S(1)}) fusion(f32[16,256]{1,0:T(8,128)S(1)} %get-tuple-element.343, f32[16,256]{1,0:T(8,128)S(1)} %get-tuple-element.344, ...), kind=kLoop, calls=%fused_computation.87 | loop fusion | flops 84910080 | bytes 360448 | tf_op jit(solution)/shard_map/reduce_sum | solution.py:83
  116.4 6.2 %multiply_reduce_fusion.17 = (f32[16,256]{1,0:T(8,128)S(1)}, f32[16,256]{1,0:T(8,128)S(1)}) fusion(f32[16,256]{1,0:T(8,128)S(1)} %get-tuple-element.347, f32[16,256]{1,0:T(8,128)S(1)} %get-tuple-element.348, f32[16,256]{1,0:T(8,128)S(1)} %get-tuple-element.333, f32[16,256]{1,0:T(8,128)S(1)} %get-tuple-element.349, f32[16,256]{1,0:T(8,128)S(1)} %get-tuple-element.334, ...), kind=kLoop, calls=%fused_computation.93 | loop fusion | flops 28303360 | bytes 163840 | tf_op jit(solution)/shard_map/reduce_sum | solution.py:83
  122.6 0.0 copy-start
  122.6 1.9 %collective-permute-start.4 = (f32[3,16,256]{2,1,0:T(8,128)S(1)}, f32[3,16,256]{2,1,0:T(8,128)S(1)}, u32[]{:S(2)}, u32[]{:S(2)}) collective-permute-start(f32[3,16,256]{2,1,0:T(8,128)S(1)} %get-tuple-element.278), channel_id=1, source_target_pairs={{7,0},{0,1},{1,2},{2,3},{3,4},{4,5},{5,6},{6,7},{15,8},{8,9},{9,10... | collective-permute-start | bytes 147464 | tf_op jit(solution)/shard_map/ppermute | solution.py:24
  124.6 2.4 %collective-permute-start.5 = (f32[3,16,256]{2,1,0:T(8,128)S(1)}, f32[3,16,256]{2,1,0:T(8,128)S(1)}, u32[]{:S(2)}, u32[]{:S(2)}) collective-permute-start(f32[3,16,256]{2,1,0:T(8,128)S(1)} %get-tuple-element.279), channel_id=1, source_target_pairs={{1,0},{2,1},{3,2},{4,3},{5,4},{6,5},{7,6},{0,7},{9,8},{10,9},{11,1... | collective-permute-start | bytes 147464 | tf_op jit(solution)/shard_map/ppermute | solution.py:24
  127.0 0.0 collective-permute-done.4
  127.0 3.2 %collective-permute-done.5 = f32[3,16,256]{2,1,0:T(8,128)S(1)} collective-permute-done((f32[3,16,256]{2,1,0:T(8,128)S(1)}, f32[3,16,256]{2,1,0:T(8,128)S(1)}, u32[]{:S(2)}, u32[]{:S(2)}) %collective-permute-start.5) | collective-permute-done | bytes 49184 | tf_op jit(solution)/shard_map/ppermute | solution.py:24
  130.2 1.9 %collective-permute-start.6 = (f32[16,1,256]{2,0,1:T(8,128)S(1)}, f32[16,1,256]{2,0,1:T(8,128)S(1)}, u32[]{:S(2)}, u32[]{:S(2)}) collective-permute-start(f32[16,1,256]{2,0,1:T(8,128)S(1)} %slice_bitcast_fusion.2), channel_id=1, source_target_pairs={{504,0},{0,8},{8,16},{16,24},{24,32},{32,40},{40,48},{48,56},{56,6... | collective-permute-start | bytes 49160 | tf_op jit(solution)/shard_map/ppermute | solution.py:24
  132.2 10.7 %collective-permute-done.6 = f32[16,1,256]{2,0,1:T(8,128)S(1)} collective-permute-done((f32[16,1,256]{2,0,1:T(8,128)S(1)}, f32[16,1,256]{2,0,1:T(8,128)S(1)}, u32[]{:S(2)}, u32[]{:S(2)}) %collective-permute-start.6) | collective-permute-done | bytes 16416 | tf_op jit(solution)/shard_map/ppermute | solution.py:24
  142.8 0.0 copy-done
  142.8 0.1 fusion.83
  142.9 0.6 copy.9
  (79 shorter events, 0.5 us)
Async XLA Ops:
  1.6 20.1 %collective-permute-start.1 = (f32[4,1,16,1,256]{4,3,2,1,0:T(1,128)S(1)}, f32[4,1,16,1,256]{4,3,2,1,0:T(1,128)S(1)}, u32[]{:S(2)}, u32[]{:S(2)}) collective-permute-start(f32[4,1,16,1,256]{4,3,2,1,0:T(1,128)S(1)} %copy_dynamic-update-slice_fusion), channel_id=1, source_target_pairs={{8,0},{16,8},{24,16},{32,24},{40,32},{48,40},{56,48},{64,56},{72,6... | collective-permute-start | bytes 196616 | tf_op jit(solution)/shard_map/ppermute | solution.py:16
  18.2 13.9 %collective-permute-start = (f32[4,1,16,1,256]{4,3,2,1,0:T(1,128)S(1)}, f32[4,1,16,1,256]{4,3,2,1,0:T(1,128)S(1)}, u32[]{:S(2)}, u32[]{:S(2)}) collective-permute-start(f32[4,1,16,1,256]{4,3,2,1,0:T(1,128)S(1)} %copy_dynamic-update-slice_fusion), channel_id=1, source_target_pairs={{0,8},{8,16},{16,24},{24,32},{32,40},{40,48},{48,56},{56,64},{64,7... | collective-permute-start | bytes 196616 | tf_op jit(solution)/shard_map/ppermute | solution.py:13
  32.2 7.9 %collective-permute-start.3 = (f32[4,3,16,1,256]{4,3,2,1,0:T(1,128)S(1)}, f32[4,3,16,1,256]{4,3,2,1,0:T(1,128)S(1)}, u32[]{:S(2)}, u32[]{:S(2)}) collective-permute-start(f32[4,3,16,1,256]{4,3,2,1,0:T(1,128)S(1)} %pad_maximum_fusion.4), channel_id=1, source_target_pairs={{0,1},{1,2},{2,3},{3,4},{4,5},{5,6},{6,7},{7,0},{8,9},{9,10},{10,1... | collective-permute-start | bytes 589832 | tf_op jit(solution)/shard_map/ppermute | solution.py:13
  37.6 7.0 %collective-permute-start.2 = (f32[4,3,16,1,256]{4,3,2,1,0:T(1,128)S(1)}, f32[4,3,16,1,256]{4,3,2,1,0:T(1,128)S(1)}, u32[]{:S(2)}, u32[]{:S(2)}) collective-permute-start(f32[4,3,16,1,256]{4,3,2,1,0:T(1,128)S(1)} %pad_maximum_fusion.4), channel_id=1, source_target_pairs={{1,0},{2,1},{3,2},{4,3},{5,4},{6,5},{7,6},{0,7},{9,8},{10,9},{11,1... | collective-permute-start | bytes 589832 | tf_op jit(solution)/shard_map/ppermute | solution.py:16
  122.6 20.2 %copy-start = (s32[1,16,1]{1,2,0:T(1,128)S(1)}, s32[1,16,1]{1,2,0:T(1,128)}, u32[]{:S(2)}) copy-start(s32[1,16,1]{1,2,0:T(1,128)} %param.38) | copy-start | bytes 196
  122.6 4.3 %collective-permute-start.4 = (f32[3,16,256]{2,1,0:T(8,128)S(1)}, f32[3,16,256]{2,1,0:T(8,128)S(1)}, u32[]{:S(2)}, u32[]{:S(2)}) collective-permute-start(f32[3,16,256]{2,1,0:T(8,128)S(1)} %get-tuple-element.278), channel_id=1, source_target_pairs={{7,0},{0,1},{1,2},{2,3},{3,4},{4,5},{5,6},{6,7},{15,8},{8,9},{9,10... | collective-permute-start | bytes 147464 | tf_op jit(solution)/shard_map/ppermute | solution.py:24
  124.6 5.6 %collective-permute-start.5 = (f32[3,16,256]{2,1,0:T(8,128)S(1)}, f32[3,16,256]{2,1,0:T(8,128)S(1)}, u32[]{:S(2)}, u32[]{:S(2)}) collective-permute-start(f32[3,16,256]{2,1,0:T(8,128)S(1)} %get-tuple-element.279), channel_id=1, source_target_pairs={{1,0},{2,1},{3,2},{4,3},{5,4},{6,5},{7,6},{0,7},{9,8},{10,9},{11,1... | collective-permute-start | bytes 147464 | tf_op jit(solution)/shard_map/ppermute | solution.py:24
  130.2 12.6 %collective-permute-start.6 = (f32[16,1,256]{2,0,1:T(8,128)S(1)}, f32[16,1,256]{2,0,1:T(8,128)S(1)}, u32[]{:S(2)}, u32[]{:S(2)}) collective-permute-start(f32[16,1,256]{2,0,1:T(8,128)S(1)} %slice_bitcast_fusion.2), channel_id=1, source_target_pairs={{504,0},{0,8},{8,16},{16,24},{24,32},{32,40},{40,48},{48,56},{56,6... | collective-permute-start | bytes 49160 | tf_op jit(solution)/shard_map/ppermute | solution.py:24
where the time goes:
time: 144 us
  other arithmetic  78.1 us (54%)
  starting transfers between devices  32 us (22%)
  waiting for transfers between devices  29.2 us (20%)
  local copies, waits for them, and re-layouts  2.73 us (2%)
  between operations  1.5 us (1%)
    reduce_sum x5, other arithmetic, shards(): density = density + jnp.sum(kernel * source_cells[3][..., None, :], axis=-1)  75.6 us
    ppermute x2, starting transfers between devices, extended_2(): lax.ppermute(lax.slice_in_dim(block, 0, width, axis=dim), axis, backward)  18.5 us
    ppermute x3, waiting for transfers between devices, shifted(): return lax.ppermute(block, axis, route)  13.8 us
    ppermute x2, waiting for transfers between devices, extended_2(): lax.ppermute(lax.slice_in_dim(block, block.shape[dim] - width, None, axis...  11 us
    ppermute x2, starting transfers between devices, extended_2(): lax.ppermute(lax.slice_in_dim(block, block.shape[dim] - width, None, axis...  7.23 us
    ppermute x3, starting transfers between devices, shifted(): return lax.ppermute(block, axis, route)  6.25 us
    ppermute x2, waiting for transfers between devices, extended_2(): lax.ppermute(lax.slice_in_dim(block, 0, width, axis=dim), axis, backward)  4.4 us
  transfers between devices with their start and end apart: 7, of which 5 were waited for; matrix products, arithmetic and copies ran while one was open for 1% of the time, Pallas kernels for 0%

commit v1 on v0

v1 whole, which is shorter than its diff:
```python
import functools

import jax
import jax.numpy as jnp
import numpy as np
from jax import lax
from jax.experimental import pallas as pl
from jax.experimental.pallas import tpu as pltpu
from jax.sharding import PartitionSpec as P

NX = 16
PS = 256
ROWS = 4480
NULL_ROW = 4416
BLOCK = 32
GROUP = 8
GAP = 48
RC = 24
STRIDE = 33
KD = 32
F32 = jnp.float32
BF16 = jnp.bfloat16

FULL = [(0, 0), (0, 1), (0, 2), (1, 0), (1, 1), (1, 2), (2, 0), (2, 1)]
SHORT = [(0, 0), (0, 1), (0, 2), (1, 0), (1, 1), (2, 0)]


def constants():
    j = np.arange(128)
    bins, cell = j // 16, j % 16
    quad, half = bins // 2, bins % 2
    place = 2 * cell + half
    rows = np.zeros((200, 128), np.float32)
    for q in range(4):
        for r in range(18):
            low, high = max(2 * (r - 1) - 1, 0), min(2 * (r - 1) + 3, 32)
            rows[q * RC + r] = (quad == q) & (place < low)
            rows[96 + q * RC + r] = (quad == q) & (place < high)
        rows[192 + q] = quad == q
    lanes = np.zeros((128, 256), np.float32)
    for q in range(4):
        for x in range(16):
            lanes[:, q * 16 + x] = (cell == x) & (quad < q)
            lanes[:, 64 + q * 16 + x] = (cell == x) & (quad == q)
            lanes[:, 128 + q * 16 + x] = (quad == q) & (cell < x)
    return jnp.asarray(rows, BF16), jnp.asarray(lanes, BF16)


def pieces(value):
    first = value.astype(BF16).astype(F32)
    rest = value - first
    second = rest.astype(BF16).astype(F32)
    return first, second, rest - second


def dot(a, b, dims=((1,), (0,))):
    return lax.dot_general(a, b, (dims, ((), ())), preferred_element_type=F32)


def prep_kernel(data, mrows, mlanes, t_out, rank_out, list_out, feat0, feat1, sorted_s, t_s, meta_v, meta_s, sem):
    y, x, z, m = data[0], data[1], data[2], data[3]
    valid = m > 0.0
    one = jnp.float32(1.0)
    nil = jnp.float32(0.0)
    code = jnp.where(y >= 0.5, 4.0, 0.0) + jnp.where(z >= 0.5, 2.0, 0.0) + jnp.where(x >= 0.5, 1.0, 0.0)
    code = jnp.where(valid, code, 9.0)
    masks = [jnp.where(code == float(b), one, nil) for b in range(8)]
    stacked = jnp.concatenate(masks, 0).astype(BF16)
    row_i = lax.broadcasted_iota(jnp.int32, (PS, PS), 0)
    lane_i = lax.broadcasted_iota(jnp.int32, (PS, PS), 1)
    upper = jnp.where(row_i <= lane_i, one, nil).astype(BF16)
    running = dot(stacked, upper)
    total = dot(stacked, jnp.ones((PS, 128), BF16))
    begin = jnp.zeros((16, 128), F32)
    rank = jnp.zeros((16, PS), F32)
    for b in range(8):
        wide = jnp.concatenate([begin, begin], 1)
        rank = rank + masks[b] * (wide + running[b * 16 : b * 16 + 16] - 1.0)
        begin = begin + total[b * 16 : b * 16 + 16]
    rank = jnp.where(valid, rank, -1.0)
    rank_out[...] = rank

    columns = dot(mrows[...], total.astype(BF16))
    base = [jnp.zeros((1, 128), F32)]
    for q in range(3):
        end = base[q] + columns[192 + q : 193 + q] + float(GAP + 15)
        base.append(jnp.floor(end * 0.0625) * 16.0)
    base_col = jnp.concatenate([jnp.broadcast_to(b, (RC, 128)) for b in base], 0)
    low, high = columns[0:96], columns[96:192]
    first = jnp.floor((low + base_col) * 0.0625) * 16.0
    n_blocks = jnp.floor((high + base_col - first + float(BLOCK - 1)) * (1.0 / BLOCK))
    n_blocks = jnp.where(high > low, n_blocks, 0.0)
    gi = lax.broadcasted_iota(jnp.int32, (96, 96), 0)
    gj = lax.broadcasted_iota(jnp.int32, (96, 96), 1)
    before = dot(jnp.where(gj < gi, one, nil).astype(BF16), n_blocks.astype(BF16))
    g128 = lax.broadcasted_iota(jnp.int32, (RC, 128), 0)
    tag = jnp.concatenate([(g128 + 32 * q).astype(F32) for q in range(4)], 0)
    null = float(NULL_ROW * 128 + 23)
    lane96 = lax.broadcasted_iota(jnp.int32, (96, 128), 1).astype(F32)
    out_rows = []
    for t in range(4):
        away = lane96 + float(128 * t) - before
        inside = (away >= 0.0) & (away < n_blocks)
        entry = (first + away * float(BLOCK)) * 128.0 + tag - null
        out_rows.append(jnp.sum(jnp.where(inside, entry, 0.0), 0, keepdims=True) + null)
    out_rows.append(before[95:96] + n_blocks[95:96])
    total_row = dot(jnp.ones((8, PS), BF16), stacked, ((1,), (1,)))
    meta = dot(total_row.astype(BF16), mlanes[...])
    lane1 = lax.broadcasted_iota(jnp.int32, (1, 128), 1)
    base_lane = jnp.where(lane1 < 16, base[0], jnp.where(lane1 < 32, base[1], jnp.where(lane1 < 48, base[2], base[3])))
    out_rows.append(meta[0:1, 0:128])
    out_rows.append(meta[0:1, 128:256] + base_lane)
    out_rows.append(jnp.zeros((1, 128), F32))
    table = jnp.concatenate(out_rows, 0).astype(jnp.int32)
    list_out[...] = table
    meta_v[...] = table
    copy = pltpu.make_async_copy(meta_v, meta_s, sem)
    copy.start()

    cell_i = lax.broadcasted_iota(jnp.int32, (16, PS), 0).astype(F32)
    xg = x + (cell_i - 8.0)
    norm = y * y + xg * xg + z * z
    py, pz, px, pn = pieces(y), pieces(z), pieces(xg), pieces(norm)
    features = [py[a] for a, _ in SHORT] + [pz[a] for a, _ in SHORT] + [px[a] for a, _ in FULL] + [pn[a] for a, _ in FULL]
    ones = jnp.ones((16, PS), F32)
    features = features + [ones, ones, ones, jnp.zeros((16, PS), F32)]
    for k in range(KD):
        feat0[pl.ds(k, 16, stride=STRIDE), :] = features[k][:, 0:128]
        feat1[pl.ds(k, 16, stride=STRIDE), :] = features[k][:, 128:256]
    t_s[...] = jnp.zeros(t_s.shape, F32)
    row_f = row_i.astype(F32)
    for c in range(16):
        place = jnp.where(row_f == rank[c : c + 1], one, nil).astype(BF16)
        both = jnp.concatenate([feat0[c * STRIDE : c * STRIDE + KD, :], feat1[c * STRIDE : c * STRIDE + KD, :]], 1)
        sorted_s[c, 0:PS, :] = dot(place, both.astype(BF16), ((1,), (1,)))
        sorted_s[c, PS : PS + 64, :] = jnp.zeros((64, KD), F32)
    copy.wait()
    for q in range(4):

        def append(c, carry, q=q):
            source = meta_s[5, q * 16 + c]
            count = meta_s[5, 64 + q * 16 + c]
            target = meta_s[6, q * 16 + c]

            def chunk(i, carry):
                t_s[pl.ds(target + 64 * i, 64), :] = sorted_s[c, pl.ds(source + 64 * i, 64), :]
                return carry

            return lax.fori_loop(0, (count + 63) // 64, chunk, carry)

        lax.fori_loop(0, 16, append, 0)
    t_out[...] = t_s[...].astype(BF16)


def pair_kernel(pencils, first_of, second_of, n_in, *refs):
    n = len(pencils)
    table, shift = refs[0], refs[1]
    inputs = refs[2 : 2 + n_in]
    targets, rank_ref, partial = refs[2 + n_in : 5 + n_in]
    out, roll_s, stage0, stage1, weights, c_lo, c_hi, acc1, acc2, d_a, d_b, back = refs[5 + n_in :]
    row_i = lax.broadcasted_iota(jnp.int32, (RC, PS), 0).astype(F32)
    acc1[...] = jnp.zeros(acc1.shape, F32)
    acc2[...] = jnp.zeros(acc2.shape, F32)
    for p, (which, index, dy, dz) in enumerate(pencils):
        start = 15 if dy == 0 else lax.rem(shift[0 if dy < 0 else 1] + 15, 16)
        rolled = []
        for f in range(4):
            value = inputs[which][index, f]
            for half in range(2):
                part = value[:, half * 128 : half * 128 + 128]
                for copy in range(3):
                    roll_s[p, 2 * f + half, copy * 16 : copy * 16 + 16, :] = part
            rolled.append(
                jnp.concatenate([roll_s[p, 2 * f, pl.ds(start, RC), :], roll_s[p, 2 * f + 1, pl.ds(start, RC), :]], 1)
            )
        y, x, z, m = rolled
        y = y + float(dy)
        z = z + float(dz)
        x = x + (row_i - 9.0)
        live = (m > 0.0) & (row_i < 18.0)
        cube = jnp.where(live, m, 1.0) * (16.0 / 3.141592653589793)
        c = jnp.where(live, jnp.exp2(jnp.log2(cube) * (1.0 / 3.0)), 0.0)
        w = c * c * 16.0
        norm = w * (y * y + x * x + z * z)
        w2 = w * -2.0
        py, pz, px, pw, pn = pieces(y * w2), pieces(z * w2), pieces(x * w2), pieces(w), pieces(norm)
        features = [py[b] for _, b in SHORT] + [pz[b] for _, b in SHORT] + [px[b] for _, b in FULL] + [pw[b] for _, b in FULL]
        features = features + list(pn) + [jnp.zeros((RC, PS), F32)]
        for k in range(KD):
            stage0[p, pl.ds(k, RC, stride=STRIDE), :] = features[k][:, 0:128]
            stage1[p, pl.ds(k, RC, stride=STRIDE), :] = features[k][:, 128:256]
        c_lo[pl.ds(p * RC, RC), :] = c[:, 0:128]
        c_hi[pl.ds(p * RC, RC), :] = c[:, 128:256]
        for r in range(RC):
            if r < 18 or r == 23:
                weights[p * RC + r, :, 0:128] = stage0[p, r * STRIDE : r * STRIDE + KD, :].astype(BF16)
                weights[p * RC + r, :, 128:256] = stage1[p, r * STRIDE : r * STRIDE + KD, :].astype(BF16)

    def decode(i):
        entry = table[lax.shift_right_logical(i, 7), lax.bitwise_and(i, 127)]
        at = pl.multiple_of(lax.shift_left(lax.shift_right_logical(entry, 11), 4), 16)
        q = lax.bitwise_and(lax.shift_right_logical(entry, 5), 3)
        r = lax.bitwise_and(entry, 31)
        return at, first_of(q) * RC + r, second_of(q) * RC + r

    def multiply(i, slot):
        at, w_a, w_b = decode(i)
        lhs = targets[pl.ds(at, BLOCK), :]
        slot[:, 0:256] = dot(lhs, weights[w_a])
        slot[:, 256:512] = dot(lhs, weights[w_b])

    def consume(i, slot):
        at, w_a, w_b = decode(i)
        cs = []
        for ref, w in ((c_lo, w_a), (c_hi, w_a), (c_lo, w_b), (c_hi, w_b)):
            cs.append(ref[pl.ds(w, 8, stride=0), :])
        for g in range(BLOCK // 8):
            sum1 = acc1[pl.ds(at + 8 * g, 8), :]
            sum2 = acc2[pl.ds(at + 8 * g, 8), :]
            for t in range(4):
                square = jnp.maximum(slot[8 * g : 8 * g + 8, 128 * t : 128 * t + 128], 1e-30)
                root = square * lax.rsqrt(square)
                inner = cs[t] - root
                outer = jnp.maximum(inner + cs[t], 0.0)
                inner = jnp.maximum(inner, 0.0)
                sum1 = sum1 + outer * outer * outer
                sum2 = sum2 + inner * inner * inner
            acc1[pl.ds(at + 8 * g, 8), :] = sum1
            acc2[pl.ds(at + 8 * g, 8), :] = sum2

    count = table[4, 0]
    for k in range(GROUP // 2):
        multiply(k, d_a.at[k])

    def step(it, carry):
        i = it * GROUP
        half = GROUP // 2
        for k in range(half):
            multiply(i + half + k, d_b.at[k])
        for k in range(half):
            consume(i + k, d_a.at[k])
        for k in range(half):
            multiply(i + GROUP + k, d_a.at[k])
        for k in range(half):
            consume(i + half + k, d_b.at[k])
        return carry

    lax.fori_loop(0, (count + GROUP - 1) // GROUP, step, 0)

    for q in range(4):

        def fetch(c, carry, q=q):
            target = table[5, q * 16 + c]
            length = table[5, 64 + q * 16 + c]
            source = table[6, q * 16 + c]

            def chunk(i, carry):
                value = acc1[pl.ds(source + 64 * i, 64), :] - 4.0 * acc2[pl.ds(source + 64 * i, 64), :]
                back[c, pl.ds(target + 64 * i, 64), :] = value
                return carry

            return lax.fori_loop(0, (length + 63) // 64, chunk, carry)

        if q == 0:
            back[...] = jnp.zeros(back.shape, F32)
        lax.fori_loop(0, 16, fetch, 0)
    row_f = lax.broadcasted_iota(jnp.int32, (PS, PS), 0).astype(F32)
    row8 = lax.broadcasted_iota(jnp.int32, (8, PS), 0)
    ones = jnp.ones((8, 128), BF16)
    for c in range(16):
        value = back[c, 0:PS, :]
        high = value.astype(BF16)
        low = (value - high.astype(F32)).astype(BF16)
        sums = dot(ones, high, ((1,), (1,))) + dot(ones, low, ((1,), (1,)))
        s1, s2, s3 = pieces(sums)
        lhs = jnp.where(row8 == 0, s1, jnp.where(row8 == 1, s2, jnp.where(row8 == 2, s3, 0.0))).astype(BF16)
        place = jnp.where(row_f == rank_ref[c : c + 1, :], 1.0, 0.0).astype(BF16)
        spread = jnp.sum(dot(lhs, place), 0, keepdims=True)
        out[c : c + 1, :] = spread + partial[c : c + 1, :]


VMEM_SPEC = pl.BlockSpec(memory_space=pltpu.VMEM)
SMEM_SPEC = pl.BlockSpec(memory_space=pltpu.SMEM)


def prepare(data, interpret=False):
    mrows, mlanes = constants()
    return pl.pallas_call(
        prep_kernel,
        out_shape=(
            jax.ShapeDtypeStruct((ROWS, KD), BF16),
            jax.ShapeDtypeStruct((NX, PS), F32),
            jax.ShapeDtypeStruct((8, 128), jnp.int32),
        ),
        in_specs=[VMEM_SPEC] * 3,
        out_specs=[VMEM_SPEC] * 3,
        scratch_shapes=[
            pltpu.VMEM((16 * STRIDE, 128), F32),
            pltpu.VMEM((16 * STRIDE, 128), F32),
            pltpu.VMEM((16, PS + 64, KD), F32),
            pltpu.VMEM((ROWS, KD), F32),
            pltpu.VMEM((8, 128), jnp.int32),
            pltpu.SMEM((8, 128), jnp.int32),
            pltpu.SemaphoreType.DMA,
        ],
        compiler_params=pltpu.CompilerParams(vmem_limit_bytes=40 << 20),
        interpret=interpret,
        name="prepare",
    )(data, mrows, mlanes)


def pair_sums(pencils, first_of, second_of, table, shift, inputs, targets, rank, partial, name, interpret=False):
    n = len(pencils)
    return pl.pallas_call(
        functools.partial(pair_kernel, pencils, first_of, second_of, len(inputs)),
        out_shape=jax.ShapeDtypeStruct((NX, PS), F32),
        in_specs=[SMEM_SPEC] * 2 + [VMEM_SPEC] * (len(inputs) + 3),
        out_specs=VMEM_SPEC,
        scratch_shapes=[
            pltpu.VMEM((n, 8, 48, 128), F32),
            pltpu.VMEM((n, RC * STRIDE, 128), F32),
            pltpu.VMEM((n, RC * STRIDE, 128), F32),
            pltpu.VMEM((n * RC, KD, PS), BF16),
            pltpu.VMEM((n * RC, 128), F32),
            pltpu.VMEM((n * RC, 128), F32),
            pltpu.VMEM((ROWS, 128), F32),
            pltpu.VMEM((ROWS, 128), F32),
            pltpu.VMEM((GROUP // 2, BLOCK, 512), F32),
            pltpu.VMEM((GROUP // 2, BLOCK, 512), F32),
            pltpu.VMEM((NX, PS + 64, 128), F32),
        ],
        compiler_params=pltpu.CompilerParams(vmem_limit_bytes=40 << 20),
        interpret=interpret,
        name=name,
    )(table, shift, *inputs, targets, rank, partial)


PENCILS_A = ((0, 0, 0, 0), (0, 1, -1, 0), (0, 2, 1, 0))
PENCILS_B = ((0, 0, 0, -1), (1, 0, 0, 1), (0, 1, -1, -1), (1, 1, -1, 1), (0, 2, 1, -1), (1, 2, 1, 1))


def near_sums(table, shift, rows, targets, rank, interpret=False):
    zero = jnp.zeros((NX, PS), F32)
    return pair_sums(
        PENCILS_A, lambda q: 0, lambda q: 1 + lax.shift_right_logical(q, 1), table, shift, [rows], targets, rank, zero, "near", interpret
    )


def far_sums(table, shift, low, high, targets, rank, partial, interpret=False):
    return pair_sums(
        PENCILS_B, lambda q: lax.bitwise_and(q, 1), lambda q: 2 + q, table, shift, [low, high], targets, rank, partial, "far", interpret
    )


def ring(axis, distance):
    count = lax.axis_size(axis)
    return [(i, (i + distance) % count) for i in range(count)]


def shards(positions, masses, counts, shear_offset):
    slot_index = lax.broadcasted_iota(jnp.int32, masses.shape, 3)
    weight = jnp.where(slot_index < counts[..., None], masses, jnp.float32(0.0))
    data = jnp.concatenate([positions, weight[None]], 0).reshape(4, NX, PS)
    index = lax.axis_index("shear")
    offset = shear_offset[0]
    shift = jnp.stack([
        jnp.where(index == 0, NX - offset, 0),
        jnp.where(index == lax.axis_size("shear") - 1, offset, 0),
    ]).astype(jnp.int32)
    below = lax.ppermute(data, "shear", ring("shear", 1))
    above = lax.ppermute(data, "shear", ring("shear", -1))
    targets, rank, table = prepare(data)
    rows = jnp.stack([data, below, above])
    low = lax.ppermute(rows, "cross", ring("cross", 1))
    high = lax.ppermute(rows, "cross", ring("cross", -1))
    partial = near_sums(table, shift, rows, targets, rank)
    density = far_sums(table, shift, low, high, targets, rank, partial)
    return density.reshape(masses.shape)


def solution(mesh):
    in_specs = (
        P(None, "shear", None, "cross", None),
        P("shear", None, "cross", None),
        P("shear", None, "cross"),
        P(),
    )
    out_specs = P("shear", None, "cross", None)
    return jax.shard_map(shards, mesh=mesh, in_specs=in_specs, out_specs=out_specs, check_vma=False)
```

time: 144 us -> 73 us (0.51)
  the two profiles are of different devices: /device:TPU:1 before, /device:TPU:62 now
where the time goes in v1:
time: 73 us; the launch traced here: 72.3 us
  Pallas kernels  35.1 us (48%)
  starting transfers between devices  19.3 us (26%)
  waiting for transfers between devices  13.1 us (18%)
  local copies, waits for them, and re-layouts  3.07 us (4%)
  other arithmetic  0.89 us (1%)
  between operations  0.77 us (1%)
    pallas_call x2, Pallas kernels, pair_sums(): pl.pallas_call(functools.partial(pair_kernel, pencils, first_of, second_o...  31.4 us
    ppermute x1, waiting for transfers between devices, shards(): above = lax.ppermute(data, 'shear', ring('shear', -1))  13.1 us
    ppermute x1, starting transfers between devices, shards(): below = lax.ppermute(data, 'shear', ring('shear', 1))  10 us
    ppermute x1, starting transfers between devices, shards(): high = lax.ppermute(rows, 'cross', ring('cross', -1))  5.44 us
    pallas_call x1, Pallas kernels, prepare(): pl.pallas_call(prep_kernel, out_shape=(jax.ShapeDtypeStruct((ROWS, KD), B...  3.74 us
    unnamed x5, local copies, waits for them, and re-layouts  2.44 us
    ppermute x1, starting transfers between devices, shards(): above = lax.ppermute(data, 'shear', ring('shear', -1))  1.92 us
    ppermute x1, starting transfers between devices, shards(): low = lax.ppermute(rows, 'cross', ring('cross', 1))  1.92 us
  transfers between devices with their start and end apart: 4, of which 1 were waited for; matrix products, arithmetic and copies ran while one was open for 0% of the time, Pallas kernels for 27%

profile of v1, /device:TPU:62, one launch (start us, length us, event | category | flops | bytes accessed | tf_op | source)
XLA Modules:
  0.0 72.3 jit_solution(7631728748503905116)
XLA Ops:
  0.0 0.8 %copy.8 = f32[3,1,16,1,256]{4,2,0,3,1:T(8,128)S(1)} copy(f32[3,1,16,1,256]{4,3,2,1,0:T(1,128)} %param.6) | data formatting | bytes 98304 | tf_op args[0]
  0.8 0.8 %fusion.2 = f32[1,1,16,1,256]{4,2,0,3,1:T(8,128)S(1)} fusion(f32[1,16,1,256]{3,2,1,0:T(1,128)} %param.7, s32[16]{0:T(128)} %bitcast.18), kind=kLoop, calls=%fused_computation.5 | loop fusion | flops 8192 | bytes 32832 | tf_op jit(solution)/shard_map/broadcast_in_dim | solution.py:363
  1.6 10.0 %collective-permute-start = (f32[4,16,256]{2,1,0:T(8,128)S(1)}, f32[4,16,256]{2,1,0:T(8,128)S(1)}, u32[]{:S(2)}, u32[]{:S(2)}) collective-permute-start(f32[4,16,256]{2,1,0:T(8,128)S(1)} %get-tuple-element.12.data), channel_id=1, source_target_pairs={{0,8},{8,16},{16,24},{24,32},{32,40},{40,48},{48,56},{56,64},{64,7... | collective-permute-start | bytes 196616 | tf_op jit(solution)/shard_map/ppermute | solution.py:370
  11.7 1.9 %collective-permute-start.1 = (f32[4,16,256]{2,1,0:T(8,128)S(1)}, f32[4,16,256]{2,1,0:T(8,128)S(1)}, u32[]{:S(2)}, u32[]{:S(2)}) collective-permute-start(f32[4,16,256]{2,1,0:T(8,128)S(1)} %get-tuple-element.12.data), channel_id=1, source_target_pairs={{0,504},{8,0},{16,8},{24,16},{32,24},{40,32},{48,40},{56,48},{64,5... | collective-permute-start | bytes 196616 | tf_op jit(solution)/shard_map/ppermute | solution.py:371
  13.6 0.0 collective-permute-done
  13.6 13.1 %collective-permute-done.1 = f32[4,16,256]{2,1,0:T(8,128)S(1)} collective-permute-done((f32[4,16,256]{2,1,0:T(8,128)S(1)}, f32[4,16,256]{2,1,0:T(8,128)S(1)}, u32[]{:S(2)}, u32[]{:S(2)}) %collective-permute-start.1) | collective-permute-done | bytes 65568 | tf_op jit(solution)/shard_map/ppermute | solution.py:371
  26.7 1.9 %collective-permute-start.2 = (f32[3,4,16,256]{3,2,1,0:T(8,128)S(1)}, f32[3,4,16,256]{3,2,1,0:T(8,128)S(1)}, u32[]{:S(2)}, u32[]{:S(2)}) collective-permute-start(f32[3,4,16,256]{3,2,1,0:T(8,128)S(1)} %pad_maximum_fusion.refs_2_), channel_id=1, source_target_pairs={{0,1},{1,2},{2,3},{3,4},{4,5},{5,6},{6,7},{7,0},{8,9},{9,10},{10,1... | collective-permute-start | bytes 589832 | tf_op jit(solution)/shard_map/ppermute | solution.py:374
  28.7 5.4 %collective-permute-start.3 = (f32[3,4,16,256]{3,2,1,0:T(8,128)S(1)}, f32[3,4,16,256]{3,2,1,0:T(8,128)S(1)}, u32[]{:S(2)}, u32[]{:S(2)}) collective-permute-start(f32[3,4,16,256]{3,2,1,0:T(8,128)S(1)} %pad_maximum_fusion.refs_2_), channel_id=1, source_target_pairs={{0,7},{1,0},{2,1},{3,2},{4,3},{5,4},{6,5},{7,6},{8,15},{9,8},{10,9... | collective-permute-start | bytes 589832 | tf_op jit(solution)/shard_map/ppermute | solution.py:375
  34.8 0.0 copy-start
  34.8 0.8 %copy-done = bf16[128,256]{1,0:T(8,128)(2,1)S(1)} copy-done((bf16[128,256]{1,0:T(8,128)(2,1)S(1)}, bf16[128,256]{1,0:T(8,128)(2,1)}, u32[]{:S(2)}) %copy-start) | copy-done | bytes 65560
  35.6 0.0 copy-start.1
  35.6 0.8 %copy-done.1 = bf16[200,128]{1,0:T(8,128)(2,1)S(1)} copy-done((bf16[200,128]{1,0:T(8,128)(2,1)S(1)}, bf16[200,128]{1,0:T(8,128)(2,1)}, u32[]{:S(2)}) %copy-start.1) | copy-done | bytes 51224
  36.4 3.7 %prepare.1 = (bf16[4480,32]{1,0:T(8,128)(2,1)S(1)}, f32[16,256]{1,0:T(8,128)S(1)}, s32[8,128]{1,0:T(8,128)S(1)}) custom-call(f32[4,16,256]{2,1,0:T(8,128)S(1)} %get-tuple-element.12.data, bf16[200,128]{1,0:T(8,128)(2,1)S(1)} %copy-done.1, bf16[128,256]{1,0:T(8,128)(2,1)S(1)} %copy-done), custom_call_target="tpu_custom_call" | custom-call | tf_op jit(solution)/shard_map/prepare/pallas_call | solution.py:288
  40.2 0.1 pad_add_fusion.refs_1_
  40.3 15.5 %near.1.refs_6_ = f32[16,256]{1,0:T(8,128)S(1)} custom-call(s32[8,128]{1,0:T(8,128)S(1)} %get-tuple-element.8.refs_0_, s32[2]{0:T(128)S(1)} %pad_add_fusion.refs_1_, f32[3,4,16,256]{3,2,1,0:T(8,128)S(1)} %pad_maximum_fusion.refs_2_, bf16[4480,32]{1,0:T(8,128)(2,1)S(1)} %get-tuple-element.9.refs_3_.refs_4_, f32[16,256]{1,0:T(8,128)S(1)} %get-tuple-element.10.refs_4_.refs_5_, ...), custom_call_target="tpu_custom_call" | custom-call | tf_op jit(solution)/shard_map/near/pallas_call | solution.py:314
  55.7 0.0 collective-permute-done.2.refs_2_
  55.7 0.0 collective-permute-done.3.refs_3_
  55.8 15.9 %far.1 = f32[16,256]{1,0:T(8,128)S(1)} custom-call(s32[8,128]{1,0:T(8,128)S(1)} %get-tuple-element.8.refs_0_, s32[2]{0:T(128)S(1)} %pad_add_fusion.refs_1_, f32[3,4,16,256]{3,2,1,0:T(8,128)S(1)} %collective-permute-done.2.refs_2_, f32[3,4,16,256]{3,2,1,0:T(8,128)S(1)} %collective-permute-done.3.refs_3_, ...), custom_call_target="tpu_custom_call" | custom-call | tf_op jit(solution)/shard_map/far/pallas_call | solution.py:314
  71.7 0.6 copy.9
  (3 shorter events, 0.0 us)
Async XLA Ops:
  1.6 12.0 %collective-permute-start = (f32[4,16,256]{2,1,0:T(8,128)S(1)}, f32[4,16,256]{2,1,0:T(8,128)S(1)}, u32[]{:S(2)}, u32[]{:S(2)}) collective-permute-start(f32[4,16,256]{2,1,0:T(8,128)S(1)} %get-tuple-element.12.data), channel_id=1, source_target_pairs={{0,8},{8,16},{16,24},{24,32},{32,40},{40,48},{48,56},{56,64},{64,7... | collective-permute-start | bytes 196616 | tf_op jit(solution)/shard_map/ppermute | solution.py:370
  11.7 15.1 %collective-permute-start.1 = (f32[4,16,256]{2,1,0:T(8,128)S(1)}, f32[4,16,256]{2,1,0:T(8,128)S(1)}, u32[]{:S(2)}, u32[]{:S(2)}) collective-permute-start(f32[4,16,256]{2,1,0:T(8,128)S(1)} %get-tuple-element.12.data), channel_id=1, source_target_pairs={{0,504},{8,0},{16,8},{24,16},{32,24},{40,32},{48,40},{56,48},{64,5... | collective-permute-start | bytes 196616 | tf_op jit(solution)/shard_map/ppermute | solution.py:371
  26.7 29.0 %collective-permute-start.2 = (f32[3,4,16,256]{3,2,1,0:T(8,128)S(1)}, f32[3,4,16,256]{3,2,1,0:T(8,128)S(1)}, u32[]{:S(2)}, u32[]{:S(2)}) collective-permute-start(f32[3,4,16,256]{3,2,1,0:T(8,128)S(1)} %pad_maximum_fusion.refs_2_), channel_id=1, source_target_pairs={{0,1},{1,2},{2,3},{3,4},{4,5},{5,6},{6,7},{7,0},{8,9},{9,10},{10,1... | collective-permute-start | bytes 589832 | tf_op jit(solution)/shard_map/ppermute | solution.py:374
  28.7 27.1 %collective-permute-start.3 = (f32[3,4,16,256]{3,2,1,0:T(8,128)S(1)}, f32[3,4,16,256]{3,2,1,0:T(8,128)S(1)}, u32[]{:S(2)}, u32[]{:S(2)}) collective-permute-start(f32[3,4,16,256]{3,2,1,0:T(8,128)S(1)} %pad_maximum_fusion.refs_2_), channel_id=1, source_target_pairs={{0,7},{1,0},{2,1},{3,2},{4,3},{5,4},{6,5},{7,6},{8,15},{9,8},{10,9... | collective-permute-start | bytes 589832 | tf_op jit(solution)/shard_map/ppermute | solution.py:375
  34.8 0.8 %copy-start = (bf16[128,256]{1,0:T(8,128)(2,1)S(1)}, bf16[128,256]{1,0:T(8,128)(2,1)}, u32[]{:S(2)}) copy-start(bf16[128,256]{1,0:T(8,128)(2,1)} %constant.20.clone.mlanes) | copy-start | bytes 196612
  35.6 0.8 %copy-start.1 = (bf16[200,128]{1,0:T(8,128)(2,1)S(1)}, bf16[200,128]{1,0:T(8,128)(2,1)}, u32[]{:S(2)}) copy-start(bf16[200,128]{1,0:T(8,128)(2,1)} %constant.19.clone.mrows) | copy-start | bytes 153604

commit v2 on v1

--- a/solution.py
+++ b/solution.py
@@ -13,8 +13,9 @@
 ROWS = 4480
 NULL_ROW = 4416
 BLOCK = 32
-GROUP = 8
+GROUP = 16
 GAP = 48
+MOVE = 96
 RC = 24
 STRIDE = 33
 KD = 32
@@ -110,7 +111,12 @@
     base_lane = jnp.where(lane1 < 16, base[0], jnp.where(lane1 < 32, base[1], jnp.where(lane1 < 48, base[2], base[3])))
     out_rows.append(meta[0:1, 0:128])
     out_rows.append(meta[0:1, 128:256] + base_lane)
-    out_rows.append(jnp.zeros((1, 128), F32))
+    longest = jnp.where(lane1 >= 64, meta[0:1, 0:128], 0.0)
+    flags = jnp.zeros((1, 128), F32)
+    for q in range(4):
+        top = jnp.max(jnp.where((lane1 >= 64 + 16 * q) & (lane1 < 80 + 16 * q), longest, 0.0), 1, keepdims=True)
+        flags = jnp.where(lane1 == q, top, flags)
+    out_rows.append(flags)
     table = jnp.concatenate(out_rows, 0).astype(jnp.int32)
     list_out[...] = table
     meta_v[...] = table
@@ -128,39 +134,56 @@
         feat0[pl.ds(k, 16, stride=STRIDE), :] = features[k][:, 0:128]
         feat1[pl.ds(k, 16, stride=STRIDE), :] = features[k][:, 128:256]
     t_s[...] = jnp.zeros(t_s.shape, F32)
-    row_f = row_i.astype(F32)
+    row_b = row_i.astype(F32).astype(BF16)
     for c in range(16):
-        place = jnp.where(row_f == rank[c : c + 1], one, nil).astype(BF16)
+        place = jnp.where(row_b == rank[c : c + 1].astype(BF16), jnp.bfloat16(1.0), jnp.bfloat16(0.0))
         both = jnp.concatenate([feat0[c * STRIDE : c * STRIDE + KD, :], feat1[c * STRIDE : c * STRIDE + KD, :]], 1)
         sorted_s[c, 0:PS, :] = dot(place, both.astype(BF16), ((1,), (1,)))
-        sorted_s[c, PS : PS + 64, :] = jnp.zeros((64, KD), F32)
+        sorted_s[c, PS : PS + MOVE, :] = jnp.zeros((MOVE, KD), F32)
     copy.wait()
     for q in range(4):
 
-        def append(c, carry, q=q):
-            source = meta_s[5, q * 16 + c]
-            count = meta_s[5, 64 + q * 16 + c]
-            target = meta_s[6, q * 16 + c]
-
-            def chunk(i, carry):
-                t_s[pl.ds(target + 64 * i, 64), :] = sorted_s[c, pl.ds(source + 64 * i, 64), :]
-                return carry
-
-            return lax.fori_loop(0, (count + 63) // 64, chunk, carry)
-
-        lax.fori_loop(0, 16, append, 0)
+        def place_of(c, q=q):
+            return meta_s[5, q * 16 + c], meta_s[5, 64 + q * 16 + c], meta_s[6, q * 16 + c]
+
+        @pl.when(meta_s[7, q] <= MOVE)
+        def _():
+            for c in range(16):
+                source, _, target = place_of(c)
+                t_s[pl.ds(target, MOVE), :] = sorted_s[c, pl.ds(source, MOVE), :]
+
+        @pl.when(meta_s[7, q] > MOVE)
+        def _():
+            def append(c, carry):
+                source, count, target = place_of(c)
+
+                def chunk(i, carry):
+                    t_s[pl.ds(target + 64 * i, 64), :] = sorted_s[c, pl.ds(source + 64 * i, 64), :]
+                    return carry
+
+                return lax.fori_loop(0, (count + 63) // 64, chunk, carry)
+
+            lax.fori_loop(0, 16, append, 0)
+
     t_out[...] = t_s[...].astype(BF16)
 
 
-def pair_kernel(pencils, first_of, second_of, n_in, *refs):
-    n = len(pencils)
+def pair_kernel(pencils, first_of, second_of, n_in, last, *refs):
     table, shift = refs[0], refs[1]
     inputs = refs[2 : 2 + n_in]
-    targets, rank_ref, partial = refs[2 + n_in : 5 + n_in]
-    out, roll_s, stage0, stage1, weights, c_lo, c_hi, acc1, acc2, d_a, d_b, back = refs[5 + n_in :]
+    targets = refs[2 + n_in]
+    refs = refs[3 + n_in :]
+    if last:
+        rank_ref, _, _, out, acc1, acc2 = refs[:6]
+        back, refs = refs[6], refs[7:]
+        back[...] = jnp.zeros(back.shape, F32)
+    else:
+        acc1, acc2 = refs[:2]
+        refs = refs[2:]
+        acc1[...] = jnp.zeros(acc1.shape, F32)
+        acc2[...] = jnp.zeros(acc2.shape, F32)
+    roll_s, stage0, stage1, weights, c_lo, c_hi, d_a, d_b = refs
     row_i = lax.broadcasted_iota(jnp.int32, (RC, PS), 0).astype(F32)
-    acc1[...] = jnp.zeros(acc1.shape, F32)
-    acc2[...] = jnp.zeros(acc2.shape, F32)
     for p, (which, index, dy, dz) in enumerate(pencils):
         start = 15 if dy == 0 else lax.rem(shift[0 if dy < 0 else 1] + 15, 16)
         rolled = []
@@ -247,24 +270,38 @@
 
     lax.fori_loop(0, (count + GROUP - 1) // GROUP, step, 0)
 
+    if last:
+        unsort(table, acc1, acc2, back, rank_ref, out)
+
+
+def unsort(table, acc1, acc2, back, rank_ref, out):
     for q in range(4):
 
-        def fetch(c, carry, q=q):
-            target = table[5, q * 16 + c]
-            length = table[5, 64 + q * 16 + c]
-            source = table[6, q * 16 + c]
-
-            def chunk(i, carry):
-                value = acc1[pl.ds(source + 64 * i, 64), :] - 4.0 * acc2[pl.ds(source + 64 * i, 64), :]
-                back[c, pl.ds(target + 64 * i, 64), :] = value
-                return carry
-
-            return lax.fori_loop(0, (length + 63) // 64, chunk, carry)
-
-        if q == 0:
-            back[...] = jnp.zeros(back.shape, F32)
-        lax.fori_loop(0, 16, fetch, 0)
-    row_f = lax.broadcasted_iota(jnp.int32, (PS, PS), 0).astype(F32)
+        def place_of(c, q=q):
+            return table[5, q * 16 + c], table[5, 64 + q * 16 + c], table[6, q * 16 + c]
+
+        @pl.when(table[7, q] <= MOVE)
+        def _():
+            for c in range(16):
+                target, _, source = place_of(c)
+                value = acc1[pl.ds(source, MOVE), :] - 4.0 * acc2[pl.ds(source, MOVE), :]
+                back[c, pl.ds(target, MOVE), :] = value
+
+        @pl.when(table[7, q] > MOVE)
+        def _():
+            def fetch(c, carry):
+                target, length, source = place_of(c)
+
+                def chunk(i, carry):
+                    value = acc1[pl.ds(source + 64 * i, 64), :] - 4.0 * acc2[pl.ds(source + 64 * i, 64), :]
+                    back[c, pl.ds(target + 64 * i, 64), :] = value
+                    return carry
+
+                return lax.fori_loop(0, (length + 63) // 64, chunk, carry)
+
+            lax.fori_loop(0, 16, fetch, 0)
+
+    row_b = lax.broadcasted_iota(jnp.int32, (PS, PS), 0).astype(F32).astype(BF16)
     row8 = lax.broadcasted_iota(jnp.int32, (8, PS), 0)
     ones = jnp.ones((8, 128), BF16)
     for c in range(16):
@@ -274,9 +311,8 @@
         sums = dot(ones, high, ((1,), (1,))) + dot(ones, low, ((1,), (1,)))
         s1, s2, s3 = pieces(sums)
         lhs = jnp.where(row8 == 0, s1, jnp.where(row8 == 1, s2, jnp.where(row8 == 2, s3, 0.0))).astype(BF16)
-        place = jnp.where(row_f == rank_ref[c : c + 1, :], 1.0, 0.0).astype(BF16)
-        spread = jnp.sum(dot(lhs, place), 0, keepdims=True)
-        out[c : c + 1, :] = spread + partial[c : c + 1, :]
+        place = jnp.where(row_b == rank_ref[c : c + 1, :].astype(BF16), jnp.bfloat16(1.0), jnp.bfloat16(0.0))
+        out[c : c + 1, :] = jnp.sum(dot(lhs, place), 0, keepdims=True)
 
 
 VMEM_SPEC = pl.BlockSpec(memory_space=pltpu.VMEM)
@@ -297,7 +333,7 @@
         scratch_shapes=[
             pltpu.VMEM((16 * STRIDE, 128), F32),
             pltpu.VMEM((16 * STRIDE, 128), F32),
-            pltpu.VMEM((16, PS + 64, KD), F32),
+            pltpu.VMEM((16, PS + MOVE, KD), F32),
             pltpu.VMEM((ROWS, KD), F32),
             pltpu.VMEM((8, 128), jnp.int32),
             pltpu.SMEM((8, 128), jnp.int32),
@@ -309,47 +345,51 @@
     )(data, mrows, mlanes)
 
 
-def pair_sums(pencils, first_of, second_of, table, shift, inputs, targets, rank, partial, name, interpret=False):
+def pair_sums(pencils, first_of, second_of, table, shift, inputs, targets, rest, name, interpret=False):
     n = len(pencils)
+    last = len(rest) > 0
+    sums = [jax.ShapeDtypeStruct((ROWS, 128), F32)] * 2
+    out_shape = [jax.ShapeDtypeStruct((NX, PS), F32)] + sums if last else sums
+    at = len(inputs) + 4
+    scratch = [
+        pltpu.VMEM((n, 8, 48, 128), F32),
+        pltpu.VMEM((n, RC * STRIDE, 128), F32),
+        pltpu.VMEM((n, RC * STRIDE, 128), F32),
+        pltpu.VMEM((n * RC, KD, PS), BF16),
+        pltpu.VMEM((n * RC, 128), F32),
+        pltpu.VMEM((n * RC, 128), F32),
+        pltpu.VMEM((GROUP // 2, BLOCK, 512), F32),
+        pltpu.VMEM((GROUP // 2, BLOCK, 512), F32),
+    ]
+    if last:
+        scratch = [pltpu.VMEM((NX, PS + MOVE, 128), F32)] + scratch
     return pl.pallas_call(
-        functools.partial(pair_kernel, pencils, first_of, second_of, len(inputs)),
-        out_shape=jax.ShapeDtypeStruct((NX, PS), F32),
-        in_specs=[SMEM_SPEC] * 2 + [VMEM_SPEC] * (len(inputs) + 3),
-        out_specs=VMEM_SPEC,
-        scratch_shapes=[
-            pltpu.VMEM((n, 8, 48, 128), F32),
-            pltpu.VMEM((n, RC * STRIDE, 128), F32),
-            pltpu.VMEM((n, RC * STRIDE, 128), F32),
-            pltpu.VMEM((n * RC, KD, PS), BF16),
-            pltpu.VMEM((n * RC, 128), F32),
-            pltpu.VMEM((n * RC, 128), F32),
-            pltpu.VMEM((ROWS, 128), F32),
-            pltpu.VMEM((ROWS, 128), F32),
-            pltpu.VMEM((GROUP // 2, BLOCK, 512), F32),
-            pltpu.VMEM((GROUP // 2, BLOCK, 512), F32),
-            pltpu.VMEM((NX, PS + 64, 128), F32),
-        ],
+        functools.partial(pair_kernel, pencils, first_of, second_of, len(inputs), last),
+        out_shape=out_shape,
+        in_specs=[SMEM_SPEC] * 2 + [VMEM_SPEC] * (len(inputs) + 1 + len(rest)),
+        out_specs=[VMEM_SPEC] * len(out_shape),
+        scratch_shapes=scratch,
+        input_output_aliases={at: 1, at + 1: 2} if last else {},
         compiler_params=pltpu.CompilerParams(vmem_limit_bytes=40 << 20),
         interpret=interpret,
         name=name,
-    )(table, shift, *inputs, targets, rank, partial)
+    )(table, shift, *inputs, targets, *rest)
 
 
 PENCILS_A = ((0, 0, 0, 0), (0, 1, -1, 0), (0, 2, 1, 0))
 PENCILS_B = ((0, 0, 0, -1), (1, 0, 0, 1), (0, 1, -1, -1), (1, 1, -1, 1), (0, 2, 1, -1), (1, 2, 1, 1))
 
 
-def near_sums(table, shift, rows, targets, rank, interpret=False):
-    zero = jnp.zeros((NX, PS), F32)
+def near_sums(table, shift, rows, targets, interpret=False):
     return pair_sums(
-        PENCILS_A, lambda q: 0, lambda q: 1 + lax.shift_right_logical(q, 1), table, shift, [rows], targets, rank, zero, "near", interpret
+        PENCILS_A, lambda q: 0, lambda q: 1 + lax.shift_right_logical(q, 1), table, shift, [rows], targets, [], "near", interpret
     )
 
 
-def far_sums(table, shift, low, high, targets, rank, partial, interpret=False):
+def far_sums(table, shift, low, high, targets, rank, sums, interpret=False):
     return pair_sums(
-        PENCILS_B, lambda q: lax.bitwise_and(q, 1), lambda q: 2 + q, table, shift, [low, high], targets, rank, partial, "far", interpret
-    )
+        PENCILS_B, lambda q: lax.bitwise_and(q, 1), lambda q: 2 + q, table, shift, [low, high], targets, [rank, *sums], "far", interpret
+    )[0]
 
 
 def ring(axis, distance):
@@ -371,10 +411,11 @@
     above = lax.ppermute(data, "shear", ring("shear", -1))
     targets, rank, table = prepare(data)
     rows = jnp.stack([data, below, above])
+    rows, targets, rank, table = lax.optimization_barrier((rows, targets, rank, table))
     low = lax.ppermute(rows, "cross", ring("cross", 1))
     high = lax.ppermute(rows, "cross", ring("cross", -1))
-    partial = near_sums(table, shift, rows, targets, rank)
-    density = far_sums(table, shift, low, high, targets, rank, partial)
+    sums = near_sums(table, shift, rows, targets)
+    density = far_sums(table, shift, low, high, targets, rank, sums)
     return density.reshape(masses.shape)
 
 

time: 73 us -> 64.9 us (0.89)
  the two profiles are of different devices: /device:TPU:62 before, /device:TPU:65 now
where the time goes in v2:
time: 64.9 us; the launch traced here: 65.1 us
  Pallas kernels  28.7 us (44%)
  starting transfers between devices  24.6 us (38%)
  waiting for transfers between devices  7.13 us (11%)
  local copies, waits for them, and re-layouts  3.06 us (5%)
  other arithmetic  0.89 us (1%)
  between operations  0.75 us (1%)
    pallas_call x2, Pallas kernels, pair_sums(): pl.pallas_call(functools.partial(pair_kernel, pencils, first_of, second_o...  26.2 us
    ppermute x1, starting transfers between devices, shards(): above = lax.ppermute(data, 'shear', ring('shear', -1))  14.8 us
    ppermute x1, waiting for transfers between devices, shards(): below = lax.ppermute(data, 'shear', ring('shear', 1))  7.12 us
    ppermute x1, starting transfers between devices, shards(): high = lax.ppermute(rows, 'cross', ring('cross', -1))  4.15 us
    ppermute x1, starting transfers between devices, shards(): low = lax.ppermute(rows, 'cross', ring('cross', 1))  3.66 us
    pallas_call x1, Pallas kernels, prepare(): pl.pallas_call(prep_kernel, out_shape=(jax.ShapeDtypeStruct((ROWS, KD), B...  2.53 us
    unnamed x5, local copies, waits for them, and re-layouts  2.44 us
    ppermute x1, starting transfers between devices, shards(): below = lax.ppermute(data, 'shear', ring('shear', 1))  1.92 us
  transfers between devices with their start and end apart: 4, of which 1 were waited for; matrix products, arithmetic and copies ran while one was open for 0% of the time, Pallas kernels for 21%

profile of v2, /device:TPU:65, one launch (start us, length us, event | category | flops | bytes accessed | tf_op | source)
XLA Modules:
  0.0 65.1 jit_solution(6478934077859958263)
XLA Ops:
  0.0 0.8 %copy.10 = f32[3,1,16,1,256]{4,2,0,3,1:T(8,128)S(1)} copy(f32[3,1,16,1,256]{4,3,2,1,0:T(1,128)} %param.6) | data formatting | bytes 98304 | tf_op args[0]
  0.8 0.8 %fusion.2 = f32[1,1,16,1,256]{4,2,0,3,1:T(8,128)S(1)} fusion(f32[1,16,1,256]{3,2,1,0:T(1,128)} %param.7, s32[16]{0:T(128)} %bitcast.18), kind=kLoop, calls=%fused_computation.5 | loop fusion | flops 8192 | bytes 32832 | tf_op jit(solution)/shard_map/broadcast_in_dim | solution.py:403
  1.6 14.8 %collective-permute-start.1 = (f32[4,16,256]{2,1,0:T(8,128)S(1)}, f32[4,16,256]{2,1,0:T(8,128)S(1)}, u32[]{:S(2)}, u32[]{:S(2)}) collective-permute-start(f32[4,16,256]{2,1,0:T(8,128)S(1)} %get-tuple-element.26.data), channel_id=1, source_target_pairs={{0,504},{8,0},{16,8},{24,16},{32,24},{40,32},{48,40},{56,48},{64,5... | collective-permute-start | bytes 196616 | tf_op jit(solution)/shard_map/ppermute | solution.py:411
  16.5 1.9 %collective-permute-start = (f32[4,16,256]{2,1,0:T(8,128)S(1)}, f32[4,16,256]{2,1,0:T(8,128)S(1)}, u32[]{:S(2)}, u32[]{:S(2)}) collective-permute-start(f32[4,16,256]{2,1,0:T(8,128)S(1)} %get-tuple-element.26.data), channel_id=1, source_target_pairs={{0,8},{8,16},{16,24},{24,32},{32,40},{40,48},{48,56},{56,64},{64,7... | collective-permute-start | bytes 196616 | tf_op jit(solution)/shard_map/ppermute | solution.py:410
  18.4 0.0 copy-start
  18.4 0.8 %copy-done = bf16[128,256]{1,0:T(8,128)(2,1)S(1)} copy-done((bf16[128,256]{1,0:T(8,128)(2,1)S(1)}, bf16[128,256]{1,0:T(8,128)(2,1)}, u32[]{:S(2)}) %copy-start) | copy-done | bytes 65560
  19.2 0.0 copy-start.1
  19.2 0.8 %copy-done.1 = bf16[200,128]{1,0:T(8,128)(2,1)S(1)} copy-done((bf16[200,128]{1,0:T(8,128)(2,1)S(1)}, bf16[200,128]{1,0:T(8,128)(2,1)}, u32[]{:S(2)}) %copy-start.1) | copy-done | bytes 51224
  20.0 2.5 %prepare.1 = (bf16[4480,32]{1,0:T(8,128)(2,1)S(1)}, f32[16,256]{1,0:T(8,128)S(1)}, s32[8,128]{1,0:T(8,128)S(1)}) custom-call(f32[4,16,256]{2,1,0:T(8,128)S(1)} %get-tuple-element.26.data, bf16[200,128]{1,0:T(8,128)(2,1)S(1)} %copy-done.1, bf16[128,256]{1,0:T(8,128)(2,1)S(1)} %copy-done), custom_call_target="tpu_custom_call" | custom-call | tf_op jit(solution)/shard_map/prepare/pallas_call | solution.py:324
  22.6 0.0 collective-permute-done.1
  22.6 7.1 %collective-permute-done = f32[4,16,256]{2,1,0:T(8,128)S(1)} collective-permute-done((f32[4,16,256]{2,1,0:T(8,128)S(1)}, f32[4,16,256]{2,1,0:T(8,128)S(1)}, u32[]{:S(2)}, u32[]{:S(2)}) %collective-permute-start) | collective-permute-done | bytes 65568 | tf_op jit(solution)/shard_map/ppermute | solution.py:410
  29.7 4.2 %collective-permute-start.3 = (f32[3,4,16,256]{3,2,1,0:T(8,128)S(1)}, f32[3,4,16,256]{3,2,1,0:T(8,128)S(1)}, u32[]{:S(2)}, u32[]{:S(2)}) collective-permute-start(f32[3,4,16,256]{3,2,1,0:T(8,128)S(1)} %pad_maximum_fusion.refs_2_), channel_id=1, source_target_pairs={{0,7},{1,0},{2,1},{3,2},{4,3},{5,4},{6,5},{7,6},{8,15},{9,8},{10,9... | collective-permute-start | bytes 589832 | tf_op jit(solution)/shard_map/ppermute | solution.py:416
  33.9 3.7 %collective-permute-start.2 = (f32[3,4,16,256]{3,2,1,0:T(8,128)S(1)}, f32[3,4,16,256]{3,2,1,0:T(8,128)S(1)}, u32[]{:S(2)}, u32[]{:S(2)}) collective-permute-start(f32[3,4,16,256]{3,2,1,0:T(8,128)S(1)} %pad_maximum_fusion.refs_2_), channel_id=1, source_target_pairs={{0,1},{1,2},{2,3},{3,4},{4,5},{5,6},{6,7},{7,0},{8,9},{9,10},{10,1... | collective-permute-start | bytes 589832 | tf_op jit(solution)/shard_map/ppermute | solution.py:415
  38.2 0.1 pad_add_fusion.refs_1_
  38.3 11.0 %near.1 = (f32[4480,128]{1,0:T(8,128)S(1)}, f32[4480,128]{1,0:T(8,128)S(1)}) custom-call(s32[8,128]{1,0:T(8,128)S(1)} %get-tuple-element.18.refs_0_, s32[2]{0:T(128)S(1)} %pad_add_fusion.refs_1_, f32[3,4,16,256]{3,2,1,0:T(8,128)S(1)} %pad_maximum_fusion.refs_2_, bf16[4480,32]{1,0:T(8,128)(2,1)S(1)} %get-tuple-element.20.refs_3_.refs_4_), custom_call_target="tpu_custom_call" | custom-call | tf_op jit(solution)/shard_map/near/pallas_call | solution.py:366
  49.3 0.0 collective-permute-done.3.refs_3_
  49.3 0.0 collective-permute-done.2.refs_2_
  49.3 15.2 %far.1 = (f32[16,256]{1,0:T(8,128)S(1)}, f32[4480,128]{1,0:T(8,128)S(1)}, f32[4480,128]{1,0:T(8,128)S(1)}) custom-call(s32[8,128]{1,0:T(8,128)S(1)} %get-tuple-element.18.refs_0_, s32[2]{0:T(128)S(1)} %pad_add_fusion.refs_1_, f32[3,4,16,256]{3,2,1,0:T(8,128)S(1)} %collective-permute-done.2.refs_2_, ...), custom_call_target="tpu_custom_call", output_to_operand_aliasing={{1}: (6, {}), {2}: (7, {})} | custom-call | tf_op jit(solution)/shard_map/far/pallas_call | solution.py:366
  64.5 0.6 copy.11
  (2 shorter events, 0.0 us)
Async XLA Ops:
  1.6 21.0 %collective-permute-start.1 = (f32[4,16,256]{2,1,0:T(8,128)S(1)}, f32[4,16,256]{2,1,0:T(8,128)S(1)}, u32[]{:S(2)}, u32[]{:S(2)}) collective-permute-start(f32[4,16,256]{2,1,0:T(8,128)S(1)} %get-tuple-element.26.data), channel_id=1, source_target_pairs={{0,504},{8,0},{16,8},{24,16},{32,24},{40,32},{48,40},{56,48},{64,5... | collective-permute-start | bytes 196616 | tf_op jit(solution)/shard_map/ppermute | solution.py:411
  16.5 13.2 %collective-permute-start = (f32[4,16,256]{2,1,0:T(8,128)S(1)}, f32[4,16,256]{2,1,0:T(8,128)S(1)}, u32[]{:S(2)}, u32[]{:S(2)}) collective-permute-start(f32[4,16,256]{2,1,0:T(8,128)S(1)} %get-tuple-element.26.data), channel_id=1, source_target_pairs={{0,8},{8,16},{16,24},{24,32},{32,40},{40,48},{48,56},{56,64},{64,7... | collective-permute-start | bytes 196616 | tf_op jit(solution)/shard_map/ppermute | solution.py:410
  18.4 0.8 %copy-start = (bf16[128,256]{1,0:T(8,128)(2,1)S(1)}, bf16[128,256]{1,0:T(8,128)(2,1)}, u32[]{:S(2)}) copy-start(bf16[128,256]{1,0:T(8,128)(2,1)} %constant.19.clone.mlanes) | copy-start | bytes 196612
  19.2 0.8 %copy-start.1 = (bf16[200,128]{1,0:T(8,128)(2,1)S(1)}, bf16[200,128]{1,0:T(8,128)(2,1)}, u32[]{:S(2)}) copy-start(bf16[200,128]{1,0:T(8,128)(2,1)} %constant.18.clone.mrows) | copy-start | bytes 153604
  29.7 19.6 %collective-permute-start.3 = (f32[3,4,16,256]{3,2,1,0:T(8,128)S(1)}, f32[3,4,16,256]{3,2,1,0:T(8,128)S(1)}, u32[]{:S(2)}, u32[]{:S(2)}) collective-permute-start(f32[3,4,16,256]{3,2,1,0:T(8,128)S(1)} %pad_maximum_fusion.refs_2_), channel_id=1, source_target_pairs={{0,7},{1,0},{2,1},{3,2},{4,3},{5,4},{6,5},{7,6},{8,15},{9,8},{10,9... | collective-permute-start | bytes 589832 | tf_op jit(solution)/shard_map/ppermute | solution.py:416
  33.9 15.4 %collective-permute-start.2 = (f32[3,4,16,256]{3,2,1,0:T(8,128)S(1)}, f32[3,4,16,256]{3,2,1,0:T(8,128)S(1)}, u32[]{:S(2)}, u32[]{:S(2)}) collective-permute-start(f32[3,4,16,256]{3,2,1,0:T(8,128)S(1)} %pad_maximum_fusion.refs_2_), channel_id=1, source_target_pairs={{0,1},{1,2},{2,3},{3,4},{4,5},{5,6},{6,7},{7,0},{8,9},{9,10},{10,1... | collective-permute-start | bytes 589832 | tf_op jit(solution)/shard_map/ppermute | solution.py:415

commit v3 on v2

--- a/solution.py
+++ b/solution.py
@@ -13,12 +13,14 @@
 ROWS = 4480
 NULL_ROW = 4416
 BLOCK = 32
-GROUP = 16
+GROUP = 8
 GAP = 48
 MOVE = 96
 RC = 24
 STRIDE = 33
 KD = 32
+ITEMS = 512
+META = 5 * ITEMS
 F32 = jnp.float32
 BF16 = jnp.bfloat16
 
@@ -94,16 +96,26 @@
     gi = lax.broadcasted_iota(jnp.int32, (96, 96), 0)
     gj = lax.broadcasted_iota(jnp.int32, (96, 96), 1)
     before = dot(jnp.where(gj < gi, one, nil).astype(BF16), n_blocks.astype(BF16))
-    g128 = lax.broadcasted_iota(jnp.int32, (RC, 128), 0)
-    tag = jnp.concatenate([(g128 + 32 * q).astype(F32) for q in range(4)], 0)
-    null = float(NULL_ROW * 128 + 23)
+    group_r = lax.broadcasted_iota(jnp.int32, (96, 128), 0)
+    group_q = group_r // RC
+    cell_r = group_r - group_q * RC
+    fields = [
+        cell_r,
+        cell_r + RC * (1 + group_q // 2),
+        cell_r + RC * lax.bitwise_and(group_q, 1),
+        cell_r + RC * (2 + group_q),
+    ]
     lane96 = lax.broadcasted_iota(jnp.int32, (96, 128), 1).astype(F32)
+    away = [lane96 + float(128 * t) - before for t in range(4)]
+    inside = [(v >= 0.0) & (v < n_blocks) for v in away]
     out_rows = []
     for t in range(4):
-        away = lane96 + float(128 * t) - before
-        inside = (away >= 0.0) & (away < n_blocks)
-        entry = (first + away * float(BLOCK)) * 128.0 + tag - null
-        out_rows.append(jnp.sum(jnp.where(inside, entry, 0.0), 0, keepdims=True) + null)
+        entry = first + away[t] * float(BLOCK) - float(NULL_ROW)
+        out_rows.append(jnp.sum(jnp.where(inside[t], entry, 0.0), 0, keepdims=True) + float(NULL_ROW))
+    for field in fields:
+        entry = field.astype(F32) - float(RC - 1)
+        for t in range(4):
+            out_rows.append(jnp.sum(jnp.where(inside[t], entry, 0.0), 0, keepdims=True) + float(RC - 1))
     out_rows.append(before[95:96] + n_blocks[95:96])
     total_row = dot(jnp.ones((8, PS), BF16), stacked, ((1,), (1,)))
     meta = dot(total_row.astype(BF16), mlanes[...])
@@ -144,15 +156,15 @@
     for q in range(4):
 
         def place_of(c, q=q):
-            return meta_s[5, q * 16 + c], meta_s[5, 64 + q * 16 + c], meta_s[6, q * 16 + c]
-
-        @pl.when(meta_s[7, q] <= MOVE)
+            return meta_s[21, q * 16 + c], meta_s[21, 64 + q * 16 + c], meta_s[22, q * 16 + c]
+
+        @pl.when(meta_s[23, q] <= MOVE)
         def _():
             for c in range(16):
                 source, _, target = place_of(c)
                 t_s[pl.ds(target, MOVE), :] = sorted_s[c, pl.ds(source, MOVE), :]
 
-        @pl.when(meta_s[7, q] > MOVE)
+        @pl.when(meta_s[23, q] > MOVE)
         def _():
             def append(c, carry):
                 source, count, target = place_of(c)
@@ -168,7 +180,7 @@
     t_out[...] = t_s[...].astype(BF16)
 
 
-def pair_kernel(pencils, first_of, second_of, n_in, last, *refs):
+def pair_kernel(pencils, first_of, n_in, last, *refs):
     table, shift = refs[0], refs[1]
     inputs = refs[2 : 2 + n_in]
     targets = refs[2 + n_in]
@@ -176,13 +188,12 @@
     if last:
         rank_ref, _, _, out, acc1, acc2 = refs[:6]
         back, refs = refs[6], refs[7:]
-        back[...] = jnp.zeros(back.shape, F32)
     else:
         acc1, acc2 = refs[:2]
         refs = refs[2:]
         acc1[...] = jnp.zeros(acc1.shape, F32)
         acc2[...] = jnp.zeros(acc2.shape, F32)
-    roll_s, stage0, stage1, weights, c_lo, c_hi, d_a, d_b = refs
+    roll_s, stage0, stage1, weights, c_lo, c_hi, squares = refs
     row_i = lax.broadcasted_iota(jnp.int32, (RC, PS), 0).astype(F32)
     for p, (which, index, dy, dz) in enumerate(pencils):
         start = 15 if dy == 0 else lax.rem(shift[0 if dy < 0 else 1] + 15, 16)
@@ -220,11 +231,7 @@
                 weights[p * RC + r, :, 128:256] = stage1[p, r * STRIDE : r * STRIDE + KD, :].astype(BF16)
 
     def decode(i):
-        entry = table[lax.shift_right_logical(i, 7), lax.bitwise_and(i, 127)]
-        at = pl.multiple_of(lax.shift_left(lax.shift_right_logical(entry, 11), 4), 16)
-        q = lax.bitwise_and(lax.shift_right_logical(entry, 5), 3)
-        r = lax.bitwise_and(entry, 31)
-        return at, first_of(q) * RC + r, second_of(q) * RC + r
+        return pl.multiple_of(table[i], 16), table[i + first_of], table[i + first_of + ITEMS]
 
     def multiply(i, slot):
         at, w_a, w_b = decode(i)
@@ -251,21 +258,16 @@
             acc1[pl.ds(at + 8 * g, 8), :] = sum1
             acc2[pl.ds(at + 8 * g, 8), :] = sum2
 
-    count = table[4, 0]
-    for k in range(GROUP // 2):
-        multiply(k, d_a.at[k])
+    count = table[META]
+    for k in range(GROUP):
+        multiply(k, squares.at[k])
 
     def step(it, carry):
         i = it * GROUP
-        half = GROUP // 2
-        for k in range(half):
-            multiply(i + half + k, d_b.at[k])
-        for k in range(half):
-            consume(i + k, d_a.at[k])
-        for k in range(half):
-            multiply(i + GROUP + k, d_a.at[k])
-        for k in range(half):
-            consume(i + half + k, d_b.at[k])
+        for k in range(GROUP):
+            consume(i + k, squares.at[k])
+        for k in range(GROUP):
+            multiply(i + GROUP + k, squares.at[k])
         return carry
 
     lax.fori_loop(0, (count + GROUP - 1) // GROUP, step, 0)
@@ -278,16 +280,17 @@
     for q in range(4):
 
         def place_of(c, q=q):
-            return table[5, q * 16 + c], table[5, 64 + q * 16 + c], table[6, q * 16 + c]
-
-        @pl.when(table[7, q] <= MOVE)
+            at = META + 128 + q * 16 + c
+            return table[at], table[at + 64], table[at + 128]
+
+        @pl.when(table[META + 384 + q] <= MOVE)
         def _():
             for c in range(16):
                 target, _, source = place_of(c)
                 value = acc1[pl.ds(source, MOVE), :] - 4.0 * acc2[pl.ds(source, MOVE), :]
                 back[c, pl.ds(target, MOVE), :] = value
 
-        @pl.when(table[7, q] > MOVE)
+        @pl.when(table[META + 384 + q] > MOVE)
         def _():
             def fetch(c, carry):
                 target, length, source = place_of(c)
@@ -301,18 +304,17 @@
 
             lax.fori_loop(0, 16, fetch, 0)
 
-    row_b = lax.broadcasted_iota(jnp.int32, (PS, PS), 0).astype(F32).astype(BF16)
-    row8 = lax.broadcasted_iota(jnp.int32, (8, PS), 0)
-    ones = jnp.ones((8, 128), BF16)
+    row_f = lax.broadcasted_iota(jnp.int32, (PS, 128), 0).astype(F32)
+    ones = jnp.ones((256, 128), BF16)
     for c in range(16):
         value = back[c, 0:PS, :]
         high = value.astype(BF16)
         low = (value - high.astype(F32)).astype(BF16)
-        sums = dot(ones, high, ((1,), (1,))) + dot(ones, low, ((1,), (1,)))
-        s1, s2, s3 = pieces(sums)
-        lhs = jnp.where(row8 == 0, s1, jnp.where(row8 == 1, s2, jnp.where(row8 == 2, s3, 0.0))).astype(BF16)
-        place = jnp.where(row_b == rank_ref[c : c + 1, :].astype(BF16), jnp.bfloat16(1.0), jnp.bfloat16(0.0))
-        out[c : c + 1, :] = jnp.sum(dot(lhs, place), 0, keepdims=True)
+        sums = dot(jnp.concatenate([high, low], 1), ones)
+        for half in range(2):
+            lanes = slice(128 * half, 128 * half + 128)
+            mine = row_f == rank_ref[c : c + 1, lanes]
+            out[c : c + 1, lanes] = jnp.sum(jnp.where(mine, sums, 0.0), 0, keepdims=True)
 
 
 VMEM_SPEC = pl.BlockSpec(memory_space=pltpu.VMEM)
@@ -326,7 +328,7 @@
         out_shape=(
             jax.ShapeDtypeStruct((ROWS, KD), BF16),
             jax.ShapeDtypeStruct((NX, PS), F32),
-            jax.ShapeDtypeStruct((8, 128), jnp.int32),
+            jax.ShapeDtypeStruct((24, 128), jnp.int32),
         ),
         in_specs=[VMEM_SPEC] * 3,
         out_specs=[VMEM_SPEC] * 3,
@@ -335,8 +337,8 @@
             pltpu.VMEM((16 * STRIDE, 128), F32),
             pltpu.VMEM((16, PS + MOVE, KD), F32),
             pltpu.VMEM((ROWS, KD), F32),
-            pltpu.VMEM((8, 128), jnp.int32),
-            pltpu.SMEM((8, 128), jnp.int32),
+            pltpu.VMEM((24, 128), jnp.int32),
+            pltpu.SMEM((24, 128), jnp.int32),
             pltpu.SemaphoreType.DMA,
         ],
         compiler_params=pltpu.CompilerParams(vmem_limit_bytes=40 << 20),
@@ -345,7 +347,7 @@
     )(data, mrows, mlanes)
 
 
-def pair_sums(pencils, first_of, second_of, table, shift, inputs, targets, rest, name, interpret=False):
+def pair_sums(pencils, first_of, table, shift, inputs, targets, rest, name, interpret=False):
     n = len(pencils)
     last = len(rest) > 0
     sums = [jax.ShapeDtypeStruct((ROWS, 128), F32)] * 2
@@ -358,13 +360,12 @@
         pltpu.VMEM((n * RC, KD, PS), BF16),
         pltpu.VMEM((n * RC, 128), F32),
         pltpu.VMEM((n * RC, 128), F32),
-        pltpu.VMEM((GROUP // 2, BLOCK, 512), F32),
-        pltpu.VMEM((GROUP // 2, BLOCK, 512), F32),
+        pltpu.VMEM((GROUP, BLOCK, 512), F32),
     ]
     if last:
         scratch = [pltpu.VMEM((NX, PS + MOVE, 128), F32)] + scratch
     return pl.pallas_call(
-        functools.partial(pair_kernel, pencils, first_of, second_of, len(inputs), last),
+        functools.partial(pair_kernel, pencils, first_of, len(inputs), last),
         out_shape=out_shape,
         in_specs=[SMEM_SPEC] * 2 + [VMEM_SPEC] * (len(inputs) + 1 + len(rest)),
         out_specs=[VMEM_SPEC] * len(out_shape),
@@ -382,13 +383,13 @@
 
 def near_sums(table, shift, rows, targets, interpret=False):
     return pair_sums(
-        PENCILS_A, lambda q: 0, lambda q: 1 + lax.shift_right_logical(q, 1), table, shift, [rows], targets, [], "near", interpret
+        PENCILS_A, ITEMS, table, shift, [rows], targets, [], "near", interpret
     )
 
 
 def far_sums(table, shift, low, high, targets, rank, sums, interpret=False):
     return pair_sums(
-        PENCILS_B, lambda q: lax.bitwise_and(q, 1), lambda q: 2 + q, table, shift, [low, high], targets, [rank, *sums], "far", interpret
+        PENCILS_B, 3 * ITEMS, table, shift, [low, high], targets, [rank, *sums], "far", interpret
     )[0]
 
 
@@ -410,6 +411,7 @@
     below = lax.ppermute(data, "shear", ring("shear", 1))
     above = lax.ppermute(data, "shear", ring("shear", -1))
     targets, rank, table = prepare(data)
+    table = table.reshape(-1)
     rows = jnp.stack([data, below, above])
     rows, targets, rank, table = lax.optimization_barrier((rows, targets, rank, table))
     low = lax.ppermute(rows, "cross", ring("cross", 1))

time: 64.9 us -> 61.4 us (0.946)
  the two profiles are of different devices: /device:TPU:65 before, /device:TPU:1 now
where the time goes in v3:
time: 61.4 us; the launch traced here: 62.3 us
  starting transfers between devices  25 us (41%)
  Pallas kernels  24.6 us (40%)
  waiting for transfers between devices  8.07 us (13%)
  local copies, waits for them, and re-layouts  3.06 us (5%)
  other arithmetic  0.89 us (1%)
  between operations  0.75 us (1%)
    pallas_call x2, Pallas kernels, pair_sums(): pl.pallas_call(functools.partial(pair_kernel, pencils, first_of, len(inpu...  22.4 us
    ppermute x1, starting transfers between devices, shards(): above = lax.ppermute(data, 'shear', ring('shear', -1))  16.6 us
    ppermute x1, waiting for transfers between devices, shards(): below = lax.ppermute(data, 'shear', ring('shear', 1))  8.06 us
    ppermute x1, starting transfers between devices, shards(): high = lax.ppermute(rows, 'cross', ring('cross', -1))  4.23 us
    unnamed x5, local copies, waits for them, and re-layouts  2.44 us
    ppermute x1, starting transfers between devices, shards(): low = lax.ppermute(rows, 'cross', ring('cross', 1))  2.29 us
    pallas_call x1, Pallas kernels, prepare(): pl.pallas_call(prep_kernel, out_shape=(jax.ShapeDtypeStruct((ROWS, KD), B...  2.21 us
    ppermute x1, starting transfers between devices, shards(): below = lax.ppermute(data, 'shear', ring('shear', 1))  1.92 us
  transfers between devices with their start and end apart: 4, of which 1 were waited for; matrix products, arithmetic and copies ran while one was open for 0% of the time, Pallas kernels for 20%

profile of v3, /device:TPU:1, one launch (start us, length us, event | category | flops | bytes accessed | tf_op | source)
XLA Modules:
  0.0 62.3 jit_solution(18138599004718095816)
XLA Ops:
  0.0 0.8 %copy.10 = f32[3,1,16,1,256]{4,2,0,3,1:T(8,128)S(1)} copy(f32[3,1,16,1,256]{4,3,2,1,0:T(1,128)} %param.6) | data formatting | bytes 98304 | tf_op args[0]
  0.8 0.8 %fusion.2 = f32[1,1,16,1,256]{4,2,0,3,1:T(8,128)S(1)} fusion(f32[1,16,1,256]{3,2,1,0:T(1,128)} %param.7, s32[16]{0:T(128)} %bitcast.21), kind=kLoop, calls=%fused_computation.5 | loop fusion | flops 8192 | bytes 32832 | tf_op jit(solution)/shard_map/broadcast_in_dim | solution.py:404
  1.6 16.6 %collective-permute-start.1 = (f32[4,16,256]{2,1,0:T(8,128)S(1)}, f32[4,16,256]{2,1,0:T(8,128)S(1)}, u32[]{:S(2)}, u32[]{:S(2)}) collective-permute-start(f32[4,16,256]{2,1,0:T(8,128)S(1)} %get-tuple-element.26.data), channel_id=1, source_target_pairs={{0,504},{8,0},{16,8},{24,16},{32,24},{40,32},{48,40},{56,48},{64,5... | collective-permute-start | bytes 196616 | tf_op jit(solution)/shard_map/ppermute | solution.py:412
  18.2 1.9 %collective-permute-start = (f32[4,16,256]{2,1,0:T(8,128)S(1)}, f32[4,16,256]{2,1,0:T(8,128)S(1)}, u32[]{:S(2)}, u32[]{:S(2)}) collective-permute-start(f32[4,16,256]{2,1,0:T(8,128)S(1)} %get-tuple-element.26.data), channel_id=1, source_target_pairs={{0,8},{8,16},{16,24},{24,32},{32,40},{40,48},{48,56},{56,64},{64,7... | collective-permute-start | bytes 196616 | tf_op jit(solution)/shard_map/ppermute | solution.py:411
  20.1 0.0 copy-start
  20.1 0.8 %copy-done = bf16[128,256]{1,0:T(8,128)(2,1)S(1)} copy-done((bf16[128,256]{1,0:T(8,128)(2,1)S(1)}, bf16[128,256]{1,0:T(8,128)(2,1)}, u32[]{:S(2)}) %copy-start) | copy-done | bytes 65560
  20.9 0.0 copy-start.1
  20.9 0.8 %copy-done.1 = bf16[200,128]{1,0:T(8,128)(2,1)S(1)} copy-done((bf16[200,128]{1,0:T(8,128)(2,1)S(1)}, bf16[200,128]{1,0:T(8,128)(2,1)}, u32[]{:S(2)}) %copy-start.1) | copy-done | bytes 51224
  21.7 2.2 %prepare.1 = (bf16[4480,32]{1,0:T(8,128)(2,1)S(1)}, f32[16,256]{1,0:T(8,128)S(1)}, s32[24,128]{1,0:T(8,128)S(1)}) custom-call(f32[4,16,256]{2,1,0:T(8,128)S(1)} %get-tuple-element.26.data, bf16[200,128]{1,0:T(8,128)(2,1)S(1)} %copy-done.1, bf16[128,256]{1,0:T(8,128)(2,1)S(1)} %copy-done), custom_call_target="tpu_custom_call" | custom-call | tf_op jit(solution)/shard_map/prepare/pallas_call | solution.py:326
  24.0 0.0 collective-permute-done.1
  24.0 8.1 %collective-permute-done = f32[4,16,256]{2,1,0:T(8,128)S(1)} collective-permute-done((f32[4,16,256]{2,1,0:T(8,128)S(1)}, f32[4,16,256]{2,1,0:T(8,128)S(1)}, u32[]{:S(2)}, u32[]{:S(2)}) %collective-permute-start) | collective-permute-done | bytes 65568 | tf_op jit(solution)/shard_map/ppermute | solution.py:411
  32.1 4.2 %collective-permute-start.3 = (f32[3,4,16,256]{3,2,1,0:T(8,128)S(1)}, f32[3,4,16,256]{3,2,1,0:T(8,128)S(1)}, u32[]{:S(2)}, u32[]{:S(2)}) collective-permute-start(f32[3,4,16,256]{3,2,1,0:T(8,128)S(1)} %pad_maximum_fusion.refs_2_), channel_id=1, source_target_pairs={{0,7},{1,0},{2,1},{3,2},{4,3},{5,4},{6,5},{7,6},{8,15},{9,8},{10,9... | collective-permute-start | bytes 589832 | tf_op jit(solution)/shard_map/ppermute | solution.py:418
  36.3 2.3 %collective-permute-start.2 = (f32[3,4,16,256]{3,2,1,0:T(8,128)S(1)}, f32[3,4,16,256]{3,2,1,0:T(8,128)S(1)}, u32[]{:S(2)}, u32[]{:S(2)}) collective-permute-start(f32[3,4,16,256]{3,2,1,0:T(8,128)S(1)} %pad_maximum_fusion.refs_2_), channel_id=1, source_target_pairs={{0,1},{1,2},{2,3},{3,4},{4,5},{5,6},{6,7},{7,0},{8,9},{9,10},{10,1... | collective-permute-start | bytes 589832 | tf_op jit(solution)/shard_map/ppermute | solution.py:417
  39.3 0.1 pad_add_fusion.refs_1_
  39.3 10.6 %near.1 = (f32[4480,128]{1,0:T(8,128)S(1)}, f32[4480,128]{1,0:T(8,128)S(1)}) custom-call(s32[3072]{0:T(1024)S(1)} %bitcast.16, s32[2]{0:T(128)S(1)} %pad_add_fusion.refs_1_, f32[3,4,16,256]{3,2,1,0:T(8,128)S(1)} %pad_maximum_fusion.refs_2_, bf16[4480,32]{1,0:T(8,128)(2,1)S(1)} %get-tuple-element.20.refs_3_.refs_4_), custom_call_target="tpu_custom_call" | custom-call | tf_op jit(solution)/shard_map/near/pallas_call | solution.py:367
  49.9 0.0 collective-permute-done.3.refs_3_
  49.9 0.0 collective-permute-done.2.refs_2_
  49.9 11.8 %far.1 = (f32[16,256]{1,0:T(8,128)S(1)}, f32[4480,128]{1,0:T(8,128)S(1)}, f32[4480,128]{1,0:T(8,128)S(1)}) custom-call(s32[3072]{0:T(1024)S(1)} %bitcast.17, s32[2]{0:T(128)S(1)} %pad_add_fusion.refs_1_, f32[3,4,16,256]{3,2,1,0:T(8,128)S(1)} %collective-permute-done.2.refs_2_, ...), custom_call_target="tpu_custom_call", output_to_operand_aliasing={{1}: (6, {}), {2}: (7, {})} | custom-call | tf_op jit(solution)/shard_map/far/pallas_call | solution.py:367
  61.7 0.6 copy.11
  (2 shorter events, 0.0 us)
Async XLA Ops:
  1.6 22.4 %collective-permute-start.1 = (f32[4,16,256]{2,1,0:T(8,128)S(1)}, f32[4,16,256]{2,1,0:T(8,128)S(1)}, u32[]{:S(2)}, u32[]{:S(2)}) collective-permute-start(f32[4,16,256]{2,1,0:T(8,128)S(1)} %get-tuple-element.26.data), channel_id=1, source_target_pairs={{0,504},{8,0},{16,8},{24,16},{32,24},{40,32},{48,40},{56,48},{64,5... | collective-permute-start | bytes 196616 | tf_op jit(solution)/shard_map/ppermute | solution.py:412
  18.2 13.9 %collective-permute-start = (f32[4,16,256]{2,1,0:T(8,128)S(1)}, f32[4,16,256]{2,1,0:T(8,128)S(1)}, u32[]{:S(2)}, u32[]{:S(2)}) collective-permute-start(f32[4,16,256]{2,1,0:T(8,128)S(1)} %get-tuple-element.26.data), channel_id=1, source_target_pairs={{0,8},{8,16},{16,24},{24,32},{32,40},{40,48},{48,56},{56,64},{64,7... | collective-permute-start | bytes 196616 | tf_op jit(solution)/shard_map/ppermute | solution.py:411
  20.1 0.8 %copy-start = (bf16[128,256]{1,0:T(8,128)(2,1)S(1)}, bf16[128,256]{1,0:T(8,128)(2,1)}, u32[]{:S(2)}) copy-start(bf16[128,256]{1,0:T(8,128)(2,1)} %constant.19.clone.mlanes) | copy-start | bytes 196612
  20.9 0.8 %copy-start.1 = (bf16[200,128]{1,0:T(8,128)(2,1)S(1)}, bf16[200,128]{1,0:T(8,128)(2,1)}, u32[]{:S(2)}) copy-start(bf16[200,128]{1,0:T(8,128)(2,1)} %constant.18.clone.mrows) | copy-start | bytes 153604
  32.1 17.8 %collective-permute-start.3 = (f32[3,4,16,256]{3,2,1,0:T(8,128)S(1)}, f32[3,4,16,256]{3,2,1,0:T(8,128)S(1)}, u32[]{:S(2)}, u32[]{:S(2)}) collective-permute-start(f32[3,4,16,256]{3,2,1,0:T(8,128)S(1)} %pad_maximum_fusion.refs_2_), channel_id=1, source_target_pairs={{0,7},{1,0},{2,1},{3,2},{4,3},{5,4},{6,5},{7,6},{8,15},{9,8},{10,9... | collective-permute-start | bytes 589832 | tf_op jit(solution)/shard_map/ppermute | solution.py:418
  36.3 13.6 %collective-permute-start.2 = (f32[3,4,16,256]{3,2,1,0:T(8,128)S(1)}, f32[3,4,16,256]{3,2,1,0:T(8,128)S(1)}, u32[]{:S(2)}, u32[]{:S(2)}) collective-permute-start(f32[3,4,16,256]{3,2,1,0:T(8,128)S(1)} %pad_maximum_fusion.refs_2_), channel_id=1, source_target_pairs={{0,1},{1,2},{2,3},{3,4},{4,5},{5,6},{6,7},{7,0},{8,9},{9,10},{10,1... | collective-permute-start | bytes 589832 | tf_op jit(solution)/shard_map/ppermute | solution.py:417

commit v4 on v3

--- a/solution.py
+++ b/solution.py
@@ -2,7 +2,6 @@
 
 import jax
 import jax.numpy as jnp
-import numpy as np
 from jax import lax
 from jax.experimental import pallas as pl
 from jax.experimental.pallas import tpu as pltpu
@@ -13,7 +12,6 @@
 ROWS = 4480
 NULL_ROW = 4416
 BLOCK = 32
-GROUP = 8
 GAP = 48
 MOVE = 96
 RC = 24
@@ -28,27 +26,6 @@
 SHORT = [(0, 0), (0, 1), (0, 2), (1, 0), (1, 1), (2, 0)]
 
 
-def constants():
-    j = np.arange(128)
-    bins, cell = j // 16, j % 16
-    quad, half = bins // 2, bins % 2
-    place = 2 * cell + half
-    rows = np.zeros((200, 128), np.float32)
-    for q in range(4):
-        for r in range(18):
-            low, high = max(2 * (r - 1) - 1, 0), min(2 * (r - 1) + 3, 32)
-            rows[q * RC + r] = (quad == q) & (place < low)
-            rows[96 + q * RC + r] = (quad == q) & (place < high)
-        rows[192 + q] = quad == q
-    lanes = np.zeros((128, 256), np.float32)
-    for q in range(4):
-        for x in range(16):
-            lanes[:, q * 16 + x] = (cell == x) & (quad < q)
-            lanes[:, 64 + q * 16 + x] = (cell == x) & (quad == q)
-            lanes[:, 128 + q * 16 + x] = (quad == q) & (cell < x)
-    return jnp.asarray(rows, BF16), jnp.asarray(lanes, BF16)
-
-
 def pieces(value):
     first = value.astype(BF16).astype(F32)
     rest = value - first
@@ -60,7 +37,11 @@
     return lax.dot_general(a, b, (dims, ((), ())), preferred_element_type=F32)
 
 
-def prep_kernel(data, mrows, mlanes, t_out, rank_out, list_out, feat0, feat1, sorted_s, t_s, meta_v, meta_s, sem):
+def steps(value, width, most):
+    return sum((value >= width * (i + 1)).astype(jnp.int32) for i in range(most))
+
+
+def prep_kernel(data, t_out, rank_out, list_out, feat0, feat1, sorted_s, t_s, meta_v, meta_s, sem):
     y, x, z, m = data[0], data[1], data[2], data[3]
     valid = m > 0.0
     one = jnp.float32(1.0)
@@ -83,7 +64,19 @@
     rank = jnp.where(valid, rank, -1.0)
     rank_out[...] = rank
 
-    columns = dot(mrows[...], total.astype(BF16))
+    g = lax.broadcasted_iota(jnp.int32, (200, 128), 0)
+    j = lax.broadcasted_iota(jnp.int32, (200, 128), 1)
+    kind = steps(g, 96, 2)
+    g = g - 96 * kind
+    group_q = steps(g, RC, 3)
+    group_x = g - RC * group_q - 1
+    limit = jnp.where(kind == 0, 2 * group_x - 1, jnp.where(group_x > 16, 0, 2 * group_x + 3))
+    limit = jnp.where((kind == 0) & (group_x > 16), 0, limit)
+    limit = jnp.where(kind == 2, 32, limit)
+    group_q = jnp.where(kind == 2, g, group_q)
+    spot = 2 * (j & 15) + ((j >> 4) & 1)
+    counted = ((j >> 5) == group_q) & (spot < limit)
+    columns = dot(jnp.where(counted, one, nil).astype(BF16), total.astype(BF16))
     base = [jnp.zeros((1, 128), F32)]
     for q in range(3):
         end = base[q] + columns[192 + q : 193 + q] + float(GAP + 15)
@@ -97,12 +90,12 @@
     gj = lax.broadcasted_iota(jnp.int32, (96, 96), 1)
     before = dot(jnp.where(gj < gi, one, nil).astype(BF16), n_blocks.astype(BF16))
     group_r = lax.broadcasted_iota(jnp.int32, (96, 128), 0)
-    group_q = group_r // RC
+    group_q = steps(group_r, RC, 3)
     cell_r = group_r - group_q * RC
     fields = [
         cell_r,
-        cell_r + RC * (1 + group_q // 2),
-        cell_r + RC * lax.bitwise_and(group_q, 1),
+        cell_r + RC * (group_q >> 1),
+        cell_r + RC * (group_q & 1),
         cell_r + RC * (2 + group_q),
     ]
     lane96 = lax.broadcasted_iota(jnp.int32, (96, 128), 1).astype(F32)
@@ -118,7 +111,13 @@
             out_rows.append(jnp.sum(jnp.where(inside[t], entry, 0.0), 0, keepdims=True) + float(RC - 1))
     out_rows.append(before[95:96] + n_blocks[95:96])
     total_row = dot(jnp.ones((8, PS), BF16), stacked, ((1,), (1,)))
-    meta = dot(total_row.astype(BF16), mlanes[...])
+    j = lax.broadcasted_iota(jnp.int32, (128, 256), 0)
+    k = lax.broadcasted_iota(jnp.int32, (128, 256), 1)
+    quad, kind, goal = j >> 5, k >> 6, (k & 63) >> 4
+    same, earlier = (j & 15) == (k & 15), (j & 15) < (k & 15)
+    counted = ((kind == 0) & same & (quad < goal)) | ((kind == 1) & same & (quad == goal))
+    counted = counted | ((kind == 2) & earlier & (quad == goal))
+    meta = dot(total_row.astype(BF16), jnp.where(counted, one, nil).astype(BF16))
     lane1 = lax.broadcasted_iota(jnp.int32, (1, 128), 1)
     base_lane = jnp.where(lane1 < 16, base[0], jnp.where(lane1 < 32, base[1], jnp.where(lane1 < 48, base[2], base[3])))
     out_rows.append(meta[0:1, 0:128])
@@ -180,14 +179,17 @@
     t_out[...] = t_s[...].astype(BF16)
 
 
-def pair_kernel(pencils, first_of, n_in, last, *refs):
+def pair_kernel(pencils, fields, group, n_in, role, *refs):
     table, shift = refs[0], refs[1]
     inputs = refs[2 : 2 + n_in]
     targets = refs[2 + n_in]
     refs = refs[3 + n_in :]
-    if last:
-        rank_ref, _, _, out, acc1, acc2 = refs[:6]
-        back, refs = refs[6], refs[7:]
+    if role == "last":
+        rank_ref, _, _, out, acc1, acc2, back = refs[:7]
+        refs = refs[7:]
+    elif role == "next":
+        acc1, acc2 = refs[2:4]
+        refs = refs[4:]
     else:
         acc1, acc2 = refs[:2]
         refs = refs[2:]
@@ -231,27 +233,25 @@
                 weights[p * RC + r, :, 128:256] = stage1[p, r * STRIDE : r * STRIDE + KD, :].astype(BF16)
 
     def decode(i):
-        return pl.multiple_of(table[i], 16), table[i + first_of], table[i + first_of + ITEMS]
+        return pl.multiple_of(table[i], 16), [table[i + ITEMS * field] for field in fields]
 
     def multiply(i, slot):
-        at, w_a, w_b = decode(i)
+        at, sources = decode(i)
         lhs = targets[pl.ds(at, BLOCK), :]
-        slot[:, 0:256] = dot(lhs, weights[w_a])
-        slot[:, 256:512] = dot(lhs, weights[w_b])
+        for n, source in enumerate(sources):
+            slot[:, 256 * n : 256 * n + 256] = dot(lhs, weights[source])
 
     def consume(i, slot):
-        at, w_a, w_b = decode(i)
-        cs = []
-        for ref, w in ((c_lo, w_a), (c_hi, w_a), (c_lo, w_b), (c_hi, w_b)):
-            cs.append(ref[pl.ds(w, 8, stride=0), :])
+        at, sources = decode(i)
+        cs = [ref[pl.ds(source, 8, stride=0), :] for source in sources for ref in (c_lo, c_hi)]
         for g in range(BLOCK // 8):
             sum1 = acc1[pl.ds(at + 8 * g, 8), :]
             sum2 = acc2[pl.ds(at + 8 * g, 8), :]
-            for t in range(4):
+            for t, scale in enumerate(cs):
                 square = jnp.maximum(slot[8 * g : 8 * g + 8, 128 * t : 128 * t + 128], 1e-30)
                 root = square * lax.rsqrt(square)
-                inner = cs[t] - root
-                outer = jnp.maximum(inner + cs[t], 0.0)
+                inner = scale - root
+                outer = jnp.maximum(inner + scale, 0.0)
                 inner = jnp.maximum(inner, 0.0)
                 sum1 = sum1 + outer * outer * outer
                 sum2 = sum2 + inner * inner * inner
@@ -259,20 +259,20 @@
             acc2[pl.ds(at + 8 * g, 8), :] = sum2
 
     count = table[META]
-    for k in range(GROUP):
+    for k in range(group):
         multiply(k, squares.at[k])
 
     def step(it, carry):
-        i = it * GROUP
-        for k in range(GROUP):
+        i = it * group
+        for k in range(group):
             consume(i + k, squares.at[k])
-        for k in range(GROUP):
-            multiply(i + GROUP + k, squares.at[k])
+        for k in range(group):
+            multiply(i + group + k, squares.at[k])
         return carry
 
-    lax.fori_loop(0, (count + GROUP - 1) // GROUP, step, 0)
-
-    if last:
+    lax.fori_loop(0, (count + group - 1) // group, step, 0)
+
+    if role == "last":
         unsort(table, acc1, acc2, back, rank_ref, out)
 
 
@@ -322,7 +322,6 @@
 
 
 def prepare(data, interpret=False):
-    mrows, mlanes = constants()
     return pl.pallas_call(
         prep_kernel,
         out_shape=(
@@ -330,7 +329,7 @@
             jax.ShapeDtypeStruct((NX, PS), F32),
             jax.ShapeDtypeStruct((24, 128), jnp.int32),
         ),
-        in_specs=[VMEM_SPEC] * 3,
+        in_specs=[VMEM_SPEC],
         out_specs=[VMEM_SPEC] * 3,
         scratch_shapes=[
             pltpu.VMEM((16 * STRIDE, 128), F32),
@@ -344,15 +343,13 @@
         compiler_params=pltpu.CompilerParams(vmem_limit_bytes=40 << 20),
         interpret=interpret,
         name="prepare",
-    )(data, mrows, mlanes)
-
-
-def pair_sums(pencils, first_of, table, shift, inputs, targets, rest, name, interpret=False):
+    )(data)
+
+
+def pair_sums(pencils, fields, group, role, table, shift, inputs, targets, rest, name, interpret=False):
     n = len(pencils)
-    last = len(rest) > 0
-    sums = [jax.ShapeDtypeStruct((ROWS, 128), F32)] * 2
-    out_shape = [jax.ShapeDtypeStruct((NX, PS), F32)] + sums if last else sums
-    at = len(inputs) + 4
+    out_shape = [jax.ShapeDtypeStruct((ROWS, 128), F32)] * 2
+    first_in, first_out = len(inputs) + 3, 0
     scratch = [
         pltpu.VMEM((n, 8, 48, 128), F32),
         pltpu.VMEM((n, RC * STRIDE, 128), F32),
@@ -360,37 +357,41 @@
         pltpu.VMEM((n * RC, KD, PS), BF16),
         pltpu.VMEM((n * RC, 128), F32),
         pltpu.VMEM((n * RC, 128), F32),
-        pltpu.VMEM((GROUP, BLOCK, 512), F32),
+        pltpu.VMEM((group, BLOCK, PS * len(fields)), F32),
     ]
-    if last:
+    if role == "last":
+        out_shape = [jax.ShapeDtypeStruct((NX, PS), F32)] + out_shape
+        first_in, first_out = first_in + 1, 1
         scratch = [pltpu.VMEM((NX, PS + MOVE, 128), F32)] + scratch
+    aliases = {} if role == "first" else {first_in: first_out, first_in + 1: first_out + 1}
     return pl.pallas_call(
-        functools.partial(pair_kernel, pencils, first_of, len(inputs), last),
+        functools.partial(pair_kernel, pencils, fields, group, len(inputs), role),
         out_shape=out_shape,
         in_specs=[SMEM_SPEC] * 2 + [VMEM_SPEC] * (len(inputs) + 1 + len(rest)),
         out_specs=[VMEM_SPEC] * len(out_shape),
         scratch_shapes=scratch,
-        input_output_aliases={at: 1, at + 1: 2} if last else {},
+        input_output_aliases=aliases,
         compiler_params=pltpu.CompilerParams(vmem_limit_bytes=40 << 20),
         interpret=interpret,
         name=name,
     )(table, shift, *inputs, targets, *rest)
 
 
-PENCILS_A = ((0, 0, 0, 0), (0, 1, -1, 0), (0, 2, 1, 0))
-PENCILS_B = ((0, 0, 0, -1), (1, 0, 0, 1), (0, 1, -1, -1), (1, 1, -1, 1), (0, 2, 1, -1), (1, 2, 1, 1))
-
-
-def near_sums(table, shift, rows, targets, interpret=False):
-    return pair_sums(
-        PENCILS_A, ITEMS, table, shift, [rows], targets, [], "near", interpret
-    )
-
-
-def far_sums(table, shift, low, high, targets, rank, sums, interpret=False):
-    return pair_sums(
-        PENCILS_B, 3 * ITEMS, table, shift, [low, high], targets, [rank, *sums], "far", interpret
-    )[0]
+OWN = ((0, 0, 0, 0),)
+SIDE = ((0, 0, -1, 0), (1, 0, 1, 0))
+FAR = ((0, 0, 0, -1), (1, 0, 0, 1), (0, 1, -1, -1), (1, 1, -1, 1), (0, 2, 1, -1), (1, 2, 1, 1))
+
+
+def own_sums(table, shift, data, targets):
+    return pair_sums(OWN, (1,), 16, "first", table, shift, [data[None]], targets, [], "own")
+
+
+def side_sums(table, shift, below, above, targets, sums):
+    return pair_sums(SIDE, (2,), 16, "next", table, shift, [below[None], above[None]], targets, sums, "side")
+
+
+def far_sums(table, shift, low, high, targets, rank, sums):
+    return pair_sums(FAR, (3, 4), 8, "last", table, shift, [low, high], targets, [rank, *sums], "far")[0]
 
 
 def ring(axis, distance):
@@ -412,11 +413,12 @@
     above = lax.ppermute(data, "shear", ring("shear", -1))
     targets, rank, table = prepare(data)
     table = table.reshape(-1)
+    sums = own_sums(table, shift, data, targets)
     rows = jnp.stack([data, below, above])
-    rows, targets, rank, table = lax.optimization_barrier((rows, targets, rank, table))
+    rows, targets, rank, table, shift, sums = lax.optimization_barrier((rows, targets, rank, table, shift, sums))
     low = lax.ppermute(rows, "cross", ring("cross", 1))
     high = lax.ppermute(rows, "cross", ring("cross", -1))
-    sums = near_sums(table, shift, rows, targets)
+    sums = side_sums(table, shift, rows[1], rows[2], targets, sums)
     density = far_sums(table, shift, low, high, targets, rank, sums)
     return density.reshape(masses.shape)
 

time: 61.4 us -> 54.8 us (0.89)
  waiting for transfers between devices: 8.07 us -> 3.3 us
  local copies, waits for them, and re-layouts: 3.06 us -> 1.44 us
    ppermute x1, waiting for transfers between devices: 8.06 us -> 3.3 us  [shards(): below = lax.ppermute(data, 'shear', ring('shear', 1))]
    unnamed x5 -> x1, local copies, waits for them, and re-layouts: 2.44 us -> 0.8 us
    pallas_call x2 -> x3, Pallas kernels: 22.4 us -> 21.5 us  [pair_sums(): pl.pallas_call(functools.partial(pair_kernel, pencils, fields, group, len...]
  transfers between devices with their start and end apart: 4 -> 4, of which waited for: 1 -> 1; matrix products, arithmetic and copies ran while one was open for 0% -> 0% of each run, Pallas kernels for 20% -> 24%
where the time goes in v4:
time: 54.8 us; the launch traced here: 55.5 us
  starting transfers between devices  25.1 us (46%)
  Pallas kernels  24 us (44%)
  waiting for transfers between devices  3.3 us (6%)
  local copies, waits for them, and re-layouts  1.44 us (3%)
  other arithmetic  0.89 us (2%)
  between operations  0.76 us (1%)
    pallas_call x3, Pallas kernels, pair_sums(): pl.pallas_call(functools.partial(pair_kernel, pencils, fields, group, len...  21.5 us
    ppermute x1, starting transfers between devices, shards(): above = lax.ppermute(data, 'shear', ring('shear', -1))  16.6 us
    ppermute x1, starting transfers between devices, shards(): high = lax.ppermute(rows, 'cross', ring('cross', -1))  3.98 us
    ppermute x1, waiting for transfers between devices, shards(): below = lax.ppermute(data, 'shear', ring('shear', 1))  3.3 us
    ppermute x1, starting transfers between devices, shards(): low = lax.ppermute(rows, 'cross', ring('cross', 1))  2.62 us
    pallas_call x1, Pallas kernels, prepare(): pl.pallas_call(prep_kernel, out_shape=(jax.ShapeDtypeStruct((ROWS, KD), B...  2.48 us
    ppermute x1, starting transfers between devices, shards(): below = lax.ppermute(data, 'shear', ring('shear', 1))  1.92 us
  transfers between devices with their start and end apart: 4, of which 1 were waited for; matrix products, arithmetic and copies ran while one was open for 0% of the time, Pallas kernels for 24%

profile of v4, /device:TPU:1, one launch (start us, length us, event | category | flops | bytes accessed | tf_op | source)
XLA Modules:
  0.0 55.5 jit_solution(16687235892673117436)
XLA Ops:
  0.0 0.8 %copy.10 = f32[3,1,16,1,256]{4,2,0,3,1:T(8,128)S(1)} copy(f32[3,1,16,1,256]{4,3,2,1,0:T(1,128)} %param.4) | data formatting | bytes 98304 | tf_op args[0]
  0.8 0.8 %fusion.2 = f32[1,1,16,1,256]{4,2,0,3,1:T(8,128)S(1)} fusion(f32[1,16,1,256]{3,2,1,0:T(1,128)} %param.5, s32[16]{0:T(128)} %bitcast.22), kind=kLoop, calls=%fused_computation.5 | loop fusion | flops 8192 | bytes 32832 | tf_op jit(solution)/shard_map/broadcast_in_dim | solution.py:405
  1.6 16.6 %collective-permute-start.1 = (f32[4,16,256]{2,1,0:T(8,128)S(1)}, f32[4,16,256]{2,1,0:T(8,128)S(1)}, u32[]{:S(2)}, u32[]{:S(2)}) collective-permute-start(f32[4,16,256]{2,1,0:T(8,128)S(1)} %get-tuple-element.38.data), channel_id=1, source_target_pairs={{0,504},{8,0},{16,8},{24,16},{32,24},{40,32},{48,40},{56,48},{64,5... | collective-permute-start | bytes 196616 | tf_op jit(solution)/shard_map/ppermute | solution.py:413
  18.2 1.9 %collective-permute-start = (f32[4,16,256]{2,1,0:T(8,128)S(1)}, f32[4,16,256]{2,1,0:T(8,128)S(1)}, u32[]{:S(2)}, u32[]{:S(2)}) collective-permute-start(f32[4,16,256]{2,1,0:T(8,128)S(1)} %get-tuple-element.38.data), channel_id=1, source_target_pairs={{0,8},{8,16},{16,24},{24,32},{32,40},{40,48},{48,56},{56,64},{64,7... | collective-permute-start | bytes 196616 | tf_op jit(solution)/shard_map/ppermute | solution.py:412
  20.1 2.5 %prepare.1 = (bf16[4480,32]{1,0:T(8,128)(2,1)S(1)}, f32[16,256]{1,0:T(8,128)S(1)}, s32[24,128]{1,0:T(8,128)S(1)}) custom-call(f32[4,16,256]{2,1,0:T(8,128)S(1)} %get-tuple-element.38.data), custom_call_target="tpu_custom_call" | custom-call | tf_op jit(solution)/shard_map/prepare/pallas_call | solution.py:325
  23.2 0.1 pad_add_fusion.refs_1_
  23.3 5.4 %own.1 = (f32[4480,128]{1,0:T(8,128)S(1)}, f32[4480,128]{1,0:T(8,128)S(1)}) custom-call(s32[3072]{0:T(1024)S(1)} %bitcast.16, s32[2]{0:T(128)S(1)} %pad_add_fusion.refs_1_, f32[1,4,16,256]{3,2,1,0:T(8,128)S(1)} %get-tuple-element.37.refs_2_, bf16[4480,32]{1,0:T(8,128)(2,1)S(1)} %get-tuple-element.28.refs_3_.refs_4_), custom_call_target="tpu_custom_call" | custom-call | tf_op jit(solution)/shard_map/own/pallas_call | solution.py:367
  28.7 0.0 collective-permute-done.1
  28.7 3.3 %collective-permute-done = f32[4,16,256]{2,1,0:T(8,128)S(1)} collective-permute-done((f32[4,16,256]{2,1,0:T(8,128)S(1)}, f32[4,16,256]{2,1,0:T(8,128)S(1)}, u32[]{:S(2)}, u32[]{:S(2)}) %collective-permute-start) | collective-permute-done | bytes 65568 | tf_op jit(solution)/shard_map/ppermute | solution.py:412
  32.0 4.0 %collective-permute-start.3 = (f32[3,4,16,256]{3,2,1,0:T(8,128)S(1)}, f32[3,4,16,256]{3,2,1,0:T(8,128)S(1)}, u32[]{:S(2)}, u32[]{:S(2)}) collective-permute-start(f32[3,4,16,256]{3,2,1,0:T(8,128)S(1)} %pad_maximum_fusion), channel_id=1, source_target_pairs={{0,7},{1,0},{2,1},{3,2},{4,3},{5,4},{6,5},{7,6},{8,15},{9,8},{10,9... | collective-permute-start | bytes 589832 | tf_op jit(solution)/shard_map/ppermute | solution.py:420
  36.0 2.6 %collective-permute-start.2 = (f32[3,4,16,256]{3,2,1,0:T(8,128)S(1)}, f32[3,4,16,256]{3,2,1,0:T(8,128)S(1)}, u32[]{:S(2)}, u32[]{:S(2)}) collective-permute-start(f32[3,4,16,256]{3,2,1,0:T(8,128)S(1)} %pad_maximum_fusion), channel_id=1, source_target_pairs={{0,1},{1,2},{2,3},{3,4},{4,5},{5,6},{6,7},{7,0},{8,9},{9,10},{10,1... | collective-permute-start | bytes 589832 | tf_op jit(solution)/shard_map/ppermute | solution.py:419
  38.7 5.2 %side.1 = (f32[4480,128]{1,0:T(8,128)S(1)}, f32[4480,128]{1,0:T(8,128)S(1)}) custom-call(s32[3072]{0:T(1024)S(1)} %bitcast.17, s32[2]{0:T(128)S(1)} %pad_add_fusion.refs_1_, f32[1,4,16,256]{3,2,1,0:T(8,128)S(1)} %get-tuple-element.36.refs_2_, f32[1,4,16,256]{3,2,1,0:T(8,128)S(1)} %get-tuple-element.35.refs_3_, ...), custom_call_target="tpu_custom_call", output_to_operand_aliasing={{0}: (5, {}), {1}: (6, {})} | custom-call | tf_op jit(solution)/shard_map/side/pallas_call | solution.py:367
  43.9 0.0 collective-permute-done.3.refs_3_
  43.9 0.0 collective-permute-done.2.refs_2_
  43.9 10.9 %far.1 = (f32[16,256]{1,0:T(8,128)S(1)}, f32[4480,128]{1,0:T(8,128)S(1)}, f32[4480,128]{1,0:T(8,128)S(1)}) custom-call(s32[3072]{0:T(1024)S(1)} %bitcast.18, s32[2]{0:T(128)S(1)} %pad_add_fusion.refs_1_, f32[3,4,16,256]{3,2,1,0:T(8,128)S(1)} %collective-permute-done.2.refs_2_, ...), custom_call_target="tpu_custom_call", output_to_operand_aliasing={{1}: (6, {}), {2}: (7, {})} | custom-call | tf_op jit(solution)/shard_map/far/pallas_call | solution.py:367
  54.8 0.6 %copy.11 = f32[1,16,1,256]{3,2,1,0:T(1,128)} copy(f32[1,16,1,256]{3,1,2,0:T(8,128)S(1)} %bitcast.19) | data formatting | bytes 32768 | tf_op jit(solution)/shard_map/reshape | solution.py:423
  (3 shorter events, 0.0 us)
Async XLA Ops:
  1.6 27.1 %collective-permute-start.1 = (f32[4,16,256]{2,1,0:T(8,128)S(1)}, f32[4,16,256]{2,1,0:T(8,128)S(1)}, u32[]{:S(2)}, u32[]{:S(2)}) collective-permute-start(f32[4,16,256]{2,1,0:T(8,128)S(1)} %get-tuple-element.38.data), channel_id=1, source_target_pairs={{0,504},{8,0},{16,8},{24,16},{32,24},{40,32},{48,40},{56,48},{64,5... | collective-permute-start | bytes 196616 | tf_op jit(solution)/shard_map/ppermute | solution.py:413
  18.2 13.8 %collective-permute-start = (f32[4,16,256]{2,1,0:T(8,128)S(1)}, f32[4,16,256]{2,1,0:T(8,128)S(1)}, u32[]{:S(2)}, u32[]{:S(2)}) collective-permute-start(f32[4,16,256]{2,1,0:T(8,128)S(1)} %get-tuple-element.38.data), channel_id=1, source_target_pairs={{0,8},{8,16},{16,24},{24,32},{32,40},{40,48},{48,56},{56,64},{64,7... | collective-permute-start | bytes 196616 | tf_op jit(solution)/shard_map/ppermute | solution.py:412
  32.0 11.9 %collective-permute-start.3 = (f32[3,4,16,256]{3,2,1,0:T(8,128)S(1)}, f32[3,4,16,256]{3,2,1,0:T(8,128)S(1)}, u32[]{:S(2)}, u32[]{:S(2)}) collective-permute-start(f32[3,4,16,256]{3,2,1,0:T(8,128)S(1)} %pad_maximum_fusion), channel_id=1, source_target_pairs={{0,7},{1,0},{2,1},{3,2},{4,3},{5,4},{6,5},{7,6},{8,15},{9,8},{10,9... | collective-permute-start | bytes 589832 | tf_op jit(solution)/shard_map/ppermute | solution.py:420
  36.0 7.9 %collective-permute-start.2 = (f32[3,4,16,256]{3,2,1,0:T(8,128)S(1)}, f32[3,4,16,256]{3,2,1,0:T(8,128)S(1)}, u32[]{:S(2)}, u32[]{:S(2)}) collective-permute-start(f32[3,4,16,256]{3,2,1,0:T(8,128)S(1)} %pad_maximum_fusion), channel_id=1, source_target_pairs={{0,1},{1,2},{2,3},{3,4},{4,5},{5,6},{6,7},{7,0},{8,9},{9,10},{10,1... | collective-permute-start | bytes 589832 | tf_op jit(solution)/shard_map/ppermute | solution.py:419

commit v5 on v4

--- a/solution.py
+++ b/solution.py
@@ -180,13 +180,19 @@
 
 
 def pair_kernel(pencils, fields, group, n_in, role, *refs):
-    table, shift = refs[0], refs[1]
     inputs = refs[2 : 2 + n_in]
+    table, shift, table_sem, shift_sem = refs[-4:]
+    table_copy = pltpu.make_async_copy(refs[0], table, table_sem)
+    shift_copy = pltpu.make_async_copy(refs[1], shift, shift_sem)
+    shift_copy.start()
+    table_copy.start()
+    shift_here = False
+    refs = refs[:-4]
     targets = refs[2 + n_in]
     refs = refs[3 + n_in :]
     if role == "last":
-        rank_ref, _, _, out, acc1, acc2, back = refs[:7]
-        refs = refs[7:]
+        rank_ref, _, _, out, acc1, acc2, back, rows_out, out_sem = refs[:9]
+        refs = refs[9:]
     elif role == "next":
         acc1, acc2 = refs[2:4]
         refs = refs[4:]
@@ -198,6 +204,9 @@
     roll_s, stage0, stage1, weights, c_lo, c_hi, squares = refs
     row_i = lax.broadcasted_iota(jnp.int32, (RC, PS), 0).astype(F32)
     for p, (which, index, dy, dz) in enumerate(pencils):
+        if dy != 0 and not shift_here:
+            shift_copy.wait()
+            shift_here = True
         start = 15 if dy == 0 else lax.rem(shift[0 if dy < 0 else 1] + 15, 16)
         rolled = []
         for f in range(4):
@@ -258,6 +267,9 @@
             acc1[pl.ds(at + 8 * g, 8), :] = sum1
             acc2[pl.ds(at + 8 * g, 8), :] = sum2
 
+    if not shift_here:
+        shift_copy.wait()
+    table_copy.wait()
     count = table[META]
     for k in range(group):
         multiply(k, squares.at[k])
@@ -273,10 +285,10 @@
     lax.fori_loop(0, (count + group - 1) // group, step, 0)
 
     if role == "last":
-        unsort(table, acc1, acc2, back, rank_ref, out)
-
-
-def unsort(table, acc1, acc2, back, rank_ref, out):
+        unsort(table, acc1, acc2, back, rank_ref, rows_out, out, out_sem)
+
+
+def unsort(table, acc1, acc2, back, rank_ref, rows_out, out, out_sem):
     for q in range(4):
 
         def place_of(c, q=q):
@@ -314,11 +326,14 @@
         for half in range(2):
             lanes = slice(128 * half, 128 * half + 128)
             mine = row_f == rank_ref[c : c + 1, lanes]
-            out[c : c + 1, lanes] = jnp.sum(jnp.where(mine, sums, 0.0), 0, keepdims=True)
+            rows_out[0, c, :, lanes] = jnp.sum(jnp.where(mine, sums, 0.0), 0, keepdims=True)
+    copy = pltpu.make_async_copy(rows_out, out, out_sem)
+    copy.start()
+    copy.wait()
 
 
 VMEM_SPEC = pl.BlockSpec(memory_space=pltpu.VMEM)
-SMEM_SPEC = pl.BlockSpec(memory_space=pltpu.SMEM)
+HBM_SPEC = pl.BlockSpec(memory_space=pl.ANY)
 
 
 def prepare(data, interpret=False):
@@ -349,6 +364,7 @@
 def pair_sums(pencils, fields, group, role, table, shift, inputs, targets, rest, name, interpret=False):
     n = len(pencils)
     out_shape = [jax.ShapeDtypeStruct((ROWS, 128), F32)] * 2
+    out_specs = [VMEM_SPEC] * 2
     first_in, first_out = len(inputs) + 3, 0
     scratch = [
         pltpu.VMEM((n, 8, 48, 128), F32),
@@ -360,15 +376,22 @@
         pltpu.VMEM((group, BLOCK, PS * len(fields)), F32),
     ]
     if role == "last":
-        out_shape = [jax.ShapeDtypeStruct((NX, PS), F32)] + out_shape
+        out_shape = [jax.ShapeDtypeStruct((1, NX, 1, PS), F32)] + out_shape
         first_in, first_out = first_in + 1, 1
-        scratch = [pltpu.VMEM((NX, PS + MOVE, 128), F32)] + scratch
+        out_specs = [HBM_SPEC] + out_specs
+        scratch = [pltpu.VMEM((NX, PS + MOVE, 128), F32), pltpu.VMEM((1, NX, 1, PS), F32), pltpu.SemaphoreType.DMA] + scratch
+    scratch = scratch + [
+        pltpu.SMEM((24 * 128,), jnp.int32),
+        pltpu.SMEM((2,), jnp.int32),
+        pltpu.SemaphoreType.DMA,
+        pltpu.SemaphoreType.DMA,
+    ]
     aliases = {} if role == "first" else {first_in: first_out, first_in + 1: first_out + 1}
     return pl.pallas_call(
         functools.partial(pair_kernel, pencils, fields, group, len(inputs), role),
         out_shape=out_shape,
-        in_specs=[SMEM_SPEC] * 2 + [VMEM_SPEC] * (len(inputs) + 1 + len(rest)),
-        out_specs=[VMEM_SPEC] * len(out_shape),
+        in_specs=[VMEM_SPEC] * (len(inputs) + 3 + len(rest)),
+        out_specs=out_specs,
         scratch_shapes=scratch,
         input_output_aliases=aliases,
         compiler_params=pltpu.CompilerParams(vmem_limit_bytes=40 << 20),
@@ -420,7 +443,7 @@
     high = lax.ppermute(rows, "cross", ring("cross", -1))
     sums = side_sums(table, shift, rows[1], rows[2], targets, sums)
     density = far_sums(table, shift, low, high, targets, rank, sums)
-    return density.reshape(masses.shape)
+    return density
 
 
 def solution(mesh):

time: 54.8 us -> 56.2 us (1.026)
  Pallas kernels: 24 us -> 26.6 us
  local copies, waits for them, and re-layouts: 1.44 us -> 0.81 us
  waiting for transfers between devices: 3.3 us -> 2.69 us
    pallas_call x3, Pallas kernels: 21.5 us -> 23.7 us  [pair_sums(): pl.pallas_call(functools.partial(pair_kernel, pencils, fields, group, len...]
    reshape x1 -> x0, local copies, waits for them, and re-layouts: 0.62 us -> none  [shards(): return density.reshape(masses.shape)]
    ppermute x1, waiting for transfers between devices: 3.3 us -> 2.68 us  [shards(): below = lax.ppermute(data, 'shear', ring('shear', 1))]
  transfers between devices with their start and end apart: 4 -> 4, of which waited for: 1 -> 1; matrix products, arithmetic and copies ran while one was open for 0% -> 0% of each run, Pallas kernels for 24% -> 25%
where the time goes in v5:
time: 56.2 us; the launch traced here: 56.8 us
  Pallas kernels  26.6 us (47%)
  starting transfers between devices  25.1 us (45%)
  waiting for transfers between devices  2.69 us (5%)
  other arithmetic  0.89 us (2%)
  local copies, waits for them, and re-layouts  0.81 us (1%)
  between operations  0.76 us (1%)
    pallas_call x3, Pallas kernels, pair_sums(): pl.pallas_call(functools.partial(pair_kernel, pencils, fields, group, len...  23.7 us
    ppermute x1, starting transfers between devices, shards(): above = lax.ppermute(data, 'shear', ring('shear', -1))  16.6 us
    ppermute x1, starting transfers between devices, shards(): high = lax.ppermute(rows, 'cross', ring('cross', -1))  3.98 us
    pallas_call x1, Pallas kernels, prepare(): pl.pallas_call(prep_kernel, out_shape=(jax.ShapeDtypeStruct((ROWS, KD), B...  2.89 us
    ppermute x1, waiting for transfers between devices, shards(): below = lax.ppermute(data, 'shear', ring('shear', 1))  2.68 us
    ppermute x1, starting transfers between devices, shards(): low = lax.ppermute(rows, 'cross', ring('cross', 1))  2.62 us
    ppermute x1, starting transfers between devices, shards(): below = lax.ppermute(data, 'shear', ring('shear', 1))  1.92 us
  transfers between devices with their start and end apart: 4, of which 1 were waited for; matrix products, arithmetic and copies ran while one was open for 0% of the time, Pallas kernels for 25%

profile of v5, /device:TPU:1, one launch (start us, length us, event | category | flops | bytes accessed | tf_op | source)
XLA Modules:
  0.0 56.8 jit_solution(15163156871016627657)
XLA Ops:
  0.0 0.8 %copy.10 = f32[3,1,16,1,256]{4,2,0,3,1:T(8,128)S(1)} copy(f32[3,1,16,1,256]{4,3,2,1,0:T(1,128)} %param.4) | data formatting | bytes 98304 | tf_op args[0]
  0.8 0.8 %fusion.2 = f32[1,1,16,1,256]{4,2,0,3,1:T(8,128)S(1)} fusion(f32[1,16,1,256]{3,2,1,0:T(1,128)} %param.5, s32[16]{0:T(128)} %bitcast.20), kind=kLoop, calls=%fused_computation.5 | loop fusion | flops 8192 | bytes 32832 | tf_op jit(solution)/shard_map/broadcast_in_dim | solution.py:428
  1.6 16.6 %collective-permute-start.1 = (f32[4,16,256]{2,1,0:T(8,128)S(1)}, f32[4,16,256]{2,1,0:T(8,128)S(1)}, u32[]{:S(2)}, u32[]{:S(2)}) collective-permute-start(f32[4,16,256]{2,1,0:T(8,128)S(1)} %get-tuple-element.38.data), channel_id=1, source_target_pairs={{0,504},{8,0},{16,8},{24,16},{32,24},{40,32},{48,40},{56,48},{64,5... | collective-permute-start | bytes 196616 | tf_op jit(solution)/shard_map/ppermute | solution.py:436
  18.2 1.9 %collective-permute-start = (f32[4,16,256]{2,1,0:T(8,128)S(1)}, f32[4,16,256]{2,1,0:T(8,128)S(1)}, u32[]{:S(2)}, u32[]{:S(2)}) collective-permute-start(f32[4,16,256]{2,1,0:T(8,128)S(1)} %get-tuple-element.38.data), channel_id=1, source_target_pairs={{0,8},{8,16},{16,24},{24,32},{32,40},{40,48},{48,56},{56,64},{64,7... | collective-permute-start | bytes 196616 | tf_op jit(solution)/shard_map/ppermute | solution.py:435
  20.1 2.9 %prepare.1 = (bf16[4480,32]{1,0:T(8,128)(2,1)S(1)}, f32[16,256]{1,0:T(8,128)S(1)}, s32[24,128]{1,0:T(8,128)S(1)}) custom-call(f32[4,16,256]{2,1,0:T(8,128)S(1)} %get-tuple-element.38.data), custom_call_target="tpu_custom_call" | custom-call | tf_op jit(solution)/shard_map/prepare/pallas_call | solution.py:340
  23.7 0.1 pad_add_fusion.refs_1_
  23.7 5.6 %own.1 = (f32[4480,128]{1,0:T(8,128)S(1)}, f32[4480,128]{1,0:T(8,128)S(1)}) custom-call(s32[3072]{0:T(1024)S(1)} %bitcast.15, s32[2]{0:T(128)S(1)} %pad_add_fusion.refs_1_, f32[1,4,16,256]{3,2,1,0:T(8,128)S(1)} %get-tuple-element.37.refs_2_, bf16[4480,32]{1,0:T(8,128)(2,1)S(1)} %get-tuple-element.28.refs_3_.refs_4_), custom_call_target="tpu_custom_call" | custom-call | tf_op jit(solution)/shard_map/own/pallas_call | solution.py:390
  29.3 0.0 collective-permute-done.1
  29.3 2.7 %collective-permute-done = f32[4,16,256]{2,1,0:T(8,128)S(1)} collective-permute-done((f32[4,16,256]{2,1,0:T(8,128)S(1)}, f32[4,16,256]{2,1,0:T(8,128)S(1)}, u32[]{:S(2)}, u32[]{:S(2)}) %collective-permute-start) | collective-permute-done | bytes 65568 | tf_op jit(solution)/shard_map/ppermute | solution.py:435
  32.0 4.0 %collective-permute-start.3 = (f32[3,4,16,256]{3,2,1,0:T(8,128)S(1)}, f32[3,4,16,256]{3,2,1,0:T(8,128)S(1)}, u32[]{:S(2)}, u32[]{:S(2)}) collective-permute-start(f32[3,4,16,256]{3,2,1,0:T(8,128)S(1)} %pad_maximum_fusion), channel_id=1, source_target_pairs={{0,7},{1,0},{2,1},{3,2},{4,3},{5,4},{6,5},{7,6},{8,15},{9,8},{10,9... | collective-permute-start | bytes 589832 | tf_op jit(solution)/shard_map/ppermute | solution.py:443
  36.0 2.6 %collective-permute-start.2 = (f32[3,4,16,256]{3,2,1,0:T(8,128)S(1)}, f32[3,4,16,256]{3,2,1,0:T(8,128)S(1)}, u32[]{:S(2)}, u32[]{:S(2)}) collective-permute-start(f32[3,4,16,256]{3,2,1,0:T(8,128)S(1)} %pad_maximum_fusion), channel_id=1, source_target_pairs={{0,1},{1,2},{2,3},{3,4},{4,5},{5,6},{6,7},{7,0},{8,9},{9,10},{10,1... | collective-permute-start | bytes 589832 | tf_op jit(solution)/shard_map/ppermute | solution.py:442
  38.7 5.7 %side.1 = (f32[4480,128]{1,0:T(8,128)S(1)}, f32[4480,128]{1,0:T(8,128)S(1)}) custom-call(s32[3072]{0:T(1024)S(1)} %bitcast.16, s32[2]{0:T(128)S(1)} %pad_add_fusion.refs_1_, f32[1,4,16,256]{3,2,1,0:T(8,128)S(1)} %get-tuple-element.36.refs_2_, f32[1,4,16,256]{3,2,1,0:T(8,128)S(1)} %get-tuple-element.35.refs_3_, ...), custom_call_target="tpu_custom_call", output_to_operand_aliasing={{0}: (5, {}), {1}: (6, {})} | custom-call | tf_op jit(solution)/shard_map/side/pallas_call | solution.py:390
  44.4 0.0 collective-permute-done.3.refs_3_
  44.4 0.0 collective-permute-done.2.refs_2_
  44.4 12.4 %far.1 = (f32[1,16,1,256]{3,2,1,0:T(1,128)}, f32[4480,128]{1,0:T(8,128)S(1)}, f32[4480,128]{1,0:T(8,128)S(1)}) custom-call(s32[3072]{0:T(1024)S(1)} %bitcast.17, s32[2]{0:T(128)S(1)} %pad_add_fusion.refs_1_, f32[3,4,16,256]{3,2,1,0:T(8,128)S(1)} %collective-permute-done.2.refs_2_, ...), custom_call_target="tpu_custom_call", output_to_operand_aliasing={{1}: (6, {}), {2}: (7, {})} | custom-call | tf_op jit(solution)/shard_map/far/pallas_call | solution.py:390
  (3 shorter events, 0.0 us)
Async XLA Ops:
  1.6 27.7 %collective-permute-start.1 = (f32[4,16,256]{2,1,0:T(8,128)S(1)}, f32[4,16,256]{2,1,0:T(8,128)S(1)}, u32[]{:S(2)}, u32[]{:S(2)}) collective-permute-start(f32[4,16,256]{2,1,0:T(8,128)S(1)} %get-tuple-element.38.data), channel_id=1, source_target_pairs={{0,504},{8,0},{16,8},{24,16},{32,24},{40,32},{48,40},{56,48},{64,5... | collective-permute-start | bytes 196616 | tf_op jit(solution)/shard_map/ppermute | solution.py:436
  18.2 13.8 %collective-permute-start = (f32[4,16,256]{2,1,0:T(8,128)S(1)}, f32[4,16,256]{2,1,0:T(8,128)S(1)}, u32[]{:S(2)}, u32[]{:S(2)}) collective-permute-start(f32[4,16,256]{2,1,0:T(8,128)S(1)} %get-tuple-element.38.data), channel_id=1, source_target_pairs={{0,8},{8,16},{16,24},{24,32},{32,40},{40,48},{48,56},{56,64},{64,7... | collective-permute-start | bytes 196616 | tf_op jit(solution)/shard_map/ppermute | solution.py:435
  32.0 12.3 %collective-permute-start.3 = (f32[3,4,16,256]{3,2,1,0:T(8,128)S(1)}, f32[3,4,16,256]{3,2,1,0:T(8,128)S(1)}, u32[]{:S(2)}, u32[]{:S(2)}) collective-permute-start(f32[3,4,16,256]{3,2,1,0:T(8,128)S(1)} %pad_maximum_fusion), channel_id=1, source_target_pairs={{0,7},{1,0},{2,1},{3,2},{4,3},{5,4},{6,5},{7,6},{8,15},{9,8},{10,9... | collective-permute-start | bytes 589832 | tf_op jit(solution)/shard_map/ppermute | solution.py:443
  36.0 8.4 %collective-permute-start.2 = (f32[3,4,16,256]{3,2,1,0:T(8,128)S(1)}, f32[3,4,16,256]{3,2,1,0:T(8,128)S(1)}, u32[]{:S(2)}, u32[]{:S(2)}) collective-permute-start(f32[3,4,16,256]{3,2,1,0:T(8,128)S(1)} %pad_maximum_fusion), channel_id=1, source_target_pairs={{0,1},{1,2},{2,3},{3,4},{4,5},{5,6},{6,7},{7,0},{8,9},{9,10},{10,1... | collective-permute-start | bytes 589832 | tf_op jit(solution)/shard_map/ppermute | solution.py:442

commit v6 on v5

--- a/solution.py
+++ b/solution.py
@@ -6,6 +6,7 @@
 from jax.experimental import pallas as pl
 from jax.experimental.pallas import tpu as pltpu
 from jax.sharding import PartitionSpec as P
+
 
 NX = 16
 PS = 256
@@ -361,7 +362,7 @@
     )(data)
 
 
-def pair_sums(pencils, fields, group, role, table, shift, inputs, targets, rest, name, interpret=False):
+def pair_sums(pencils, fields, group, role, table, shift, inputs, targets, rest, interpret=False):
     n = len(pencils)
     out_shape = [jax.ShapeDtypeStruct((ROWS, 128), F32)] * 2
     out_specs = [VMEM_SPEC] * 2
@@ -396,7 +397,6 @@
         input_output_aliases=aliases,
         compiler_params=pltpu.CompilerParams(vmem_limit_bytes=40 << 20),
         interpret=interpret,
-        name=name,
     )(table, shift, *inputs, targets, *rest)
 
 
@@ -406,15 +406,15 @@
 
 
 def own_sums(table, shift, data, targets):
-    return pair_sums(OWN, (1,), 16, "first", table, shift, [data[None]], targets, [], "own")
+    return pair_sums(OWN, (1,), 16, "first", table, shift, [data[None]], targets, [])
 
 
 def side_sums(table, shift, below, above, targets, sums):
-    return pair_sums(SIDE, (2,), 16, "next", table, shift, [below[None], above[None]], targets, sums, "side")
+    return pair_sums(SIDE, (2,), 16, "next", table, shift, [below[None], above[None]], targets, sums)
 
 
 def far_sums(table, shift, low, high, targets, rank, sums):
-    return pair_sums(FAR, (3, 4), 8, "last", table, shift, [low, high], targets, [rank, *sums], "far")[0]
+    return pair_sums(FAR, (3, 4), 8, "last", table, shift, [low, high], targets, [rank, *sums])[0]
 
 
 def ring(axis, distance):
@@ -432,11 +432,18 @@
         jnp.where(index == 0, NX - offset, 0),
         jnp.where(index == lax.axis_size("shear") - 1, offset, 0),
     ]).astype(jnp.int32)
-    below = lax.ppermute(data, "shear", ring("shear", 1))
-    above = lax.ppermute(data, "shear", ring("shear", -1))
+    n_rows = lax.axis_size("shear")
+    half = n_rows // 2
+    ends = [(i, (i + 1) % n_rows) for i in (half - 1, n_rows - 1)]
+    inner = [(i, i + 1) for i in range(n_rows) if (i, (i + 1) % n_rows) not in ends]
+    distant = lax.ppermute(data, "shear", ends + [(j, i) for i, j in ends])
+    below = lax.ppermute(data, "shear", inner)
+    above = lax.ppermute(data, "shear", [(j, i) for i, j in inner])
     targets, rank, table = prepare(data)
     table = table.reshape(-1)
     sums = own_sums(table, shift, data, targets)
+    below = jnp.where(lax.rem(index, half) == 0, distant, below)
+    above = jnp.where(lax.rem(index, half) == half - 1, distant, above)
     rows = jnp.stack([data, below, above])
     rows, targets, rank, table, shift, sums = lax.optimization_barrier((rows, targets, rank, table, shift, sums))
     low = lax.ppermute(rows, "cross", ring("cross", 1))

time: 56.2 us -> 51.9 us (0.923); the launches traced: 56.8 us -> 51.6 us
  Pallas kernels: 26.6 us -> 23 us
  waiting for transfers between devices: 2.69 us -> 0.01 us
  starting transfers between devices: 25.1 us -> 26.1 us
    pallas_call x3, Pallas kernels: 23.7 us -> 20.1 us  [pair_sums(): pl.pallas_call(functools.partial(pair_kernel, pencils, fields, group, len...]
    ppermute x2 -> x3, waiting for transfers between devices: 2.69 us -> 0.01 us  [the longest x1 0.01 us: shards(): above = lax.ppermute(data, 'shear', [(j, i) for i, j in inner])]
    ppermute x2 -> x3, starting transfers between devices: 18.5 us -> 20.3 us  [the longest x1 14.4 us: shards(): distant = lax.ppermute(data, 'shear', ends + [(j, i) for i, j in ends])]
    ppermute x1, starting transfers between devices: 3.98 us -> 3.14 us  [shards(): high = lax.ppermute(rows, 'cross', ring('cross', -1))]
  transfers between devices with their start and end apart: 4 -> 5, of which waited for: 1 -> 0; matrix products, arithmetic and copies ran while one was open for 0% -> 0% of each run, Pallas kernels for 25% -> 24%
where the time goes in v6:
time: 51.9 us; the launch traced here: 51.6 us
  starting transfers between devices  26.1 us (50%)
  Pallas kernels  23 us (44%)
  other arithmetic  0.91 us (2%)
  local copies, waits for them, and re-layouts  0.81 us (2%)
  between operations  0.8 us (2%)
    pallas_call x3, Pallas kernels, pair_sums(): pl.pallas_call(functools.partial(pair_kernel, pencils, fields, group, len...  20.1 us
    ppermute x1, starting transfers between devices, shards(): distant = lax.ppermute(data, 'shear', ends + [(j, i) for i, j in ends])  14.4 us
    ppermute x1, starting transfers between devices, shards(): below = lax.ppermute(data, 'shear', inner)  4.56 us
    ppermute x1, starting transfers between devices, shards(): high = lax.ppermute(rows, 'cross', ring('cross', -1))  3.14 us
    pallas_call x1, Pallas kernels, prepare(): pl.pallas_call(prep_kernel, out_shape=(jax.ShapeDtypeStruct((ROWS, KD), B...  2.88 us
    ppermute x1, starting transfers between devices, shards(): low = lax.ppermute(rows, 'cross', ring('cross', 1))  2.65 us
    ppermute x1, starting transfers between devices, shards(): above = lax.ppermute(data, 'shear', [(j, i) for i, j in inner])  1.29 us
  transfers between devices with their start and end apart: 5, of which 0 were waited for; matrix products, arithmetic and copies ran while one was open for 0% of the time, Pallas kernels for 24%

profile of v6, /device:TPU:1, one launch (start us, length us, event | category | flops | bytes accessed | tf_op | source)
XLA Modules:
  0.0 51.6 jit_solution(1340448612711125785)
XLA Ops:
  0.0 0.8 %copy.10 = f32[3,1,16,1,256]{4,2,0,3,1:T(8,128)S(1)} copy(f32[3,1,16,1,256]{4,3,2,1,0:T(1,128)} %param.4) | data formatting | bytes 98304 | tf_op args[0]
  0.8 0.8 %fusion.2 = f32[1,1,16,1,256]{4,2,0,3,1:T(8,128)S(1)} fusion(f32[1,16,1,256]{3,2,1,0:T(1,128)} %param.5, s32[16]{0:T(128)} %bitcast.20), kind=kLoop, calls=%fused_computation.7 | loop fusion | flops 8192 | bytes 32832 | tf_op jit(solution)/shard_map/broadcast_in_dim | solution.py:428
  1.6 1.3 %collective-permute-start.2 = (f32[4,16,256]{2,1,0:T(8,128)S(1)}, f32[4,16,256]{2,1,0:T(8,128)S(1)}, u32[]{:S(2)}, u32[]{:S(2)}) collective-permute-start(f32[4,16,256]{2,1,0:T(8,128)S(1)} %get-tuple-element.38.data), channel_id=1, source_target_pairs={{8,0},{16,8},{24,16},{32,24},{40,32},{48,40},{56,48},{64,56},{72,6... | collective-permute-start | bytes 196616 | tf_op jit(solution)/shard_map/ppermute | solution.py:441
  2.9 4.6 %collective-permute-start.1 = (f32[4,16,256]{2,1,0:T(8,128)S(1)}, f32[4,16,256]{2,1,0:T(8,128)S(1)}, u32[]{:S(2)}, u32[]{:S(2)}) collective-permute-start(f32[4,16,256]{2,1,0:T(8,128)S(1)} %get-tuple-element.38.data), channel_id=1, source_target_pairs={{0,8},{8,16},{16,24},{24,32},{32,40},{40,48},{48,56},{56,64},{64,7... | collective-permute-start | bytes 196616 | tf_op jit(solution)/shard_map/ppermute | solution.py:440
  7.5 14.4 %collective-permute-start = (f32[4,16,256]{2,1,0:T(8,128)S(1)}, f32[4,16,256]{2,1,0:T(8,128)S(1)}, u32[]{:S(2)}, u32[]{:S(2)}) collective-permute-start(f32[4,16,256]{2,1,0:T(8,128)S(1)} %get-tuple-element.38.data), channel_id=1, source_target_pairs={{248,256},{504,0},{256,248},{0,504},{249,257},{505,1},{257,249},{1... | collective-permute-start | bytes 196616 | tf_op jit(solution)/shard_map/ppermute | solution.py:439
  21.9 2.9 %prepare.1 = (bf16[4480,32]{1,0:T(8,128)(2,1)S(1)}, f32[16,256]{1,0:T(8,128)S(1)}, s32[24,128]{1,0:T(8,128)S(1)}) custom-call(f32[4,16,256]{2,1,0:T(8,128)S(1)} %get-tuple-element.38.data), custom_call_target="tpu_custom_call" | custom-call | tf_op jit(solution)/shard_map/prepare/pallas_call | solution.py:341
  25.5 0.1 pad_add_fusion.refs_1_
  25.6 4.7 %shard_map.49 = (f32[4480,128]{1,0:T(8,128)S(1)}, f32[4480,128]{1,0:T(8,128)S(1)}) custom-call(s32[3072]{0:T(1024)S(1)} %bitcast.17, s32[2]{0:T(128)S(1)} %pad_add_fusion.refs_1_, f32[1,4,16,256]{3,2,1,0:T(8,128)S(1)} %get-tuple-element.37.refs_2_, bf16[4480,32]{1,0:T(8,128)(2,1)S(1)} %get-tuple-element.28.refs_3_.refs_4_), custom_call_target="tpu_custom_call" | custom-call | tf_op jit(solution)/shard_map/pallas_call | solution.py:391
  30.3 0.0 collective-permute-done.2
  30.3 0.0 collective-permute-done.1
  30.3 0.0 collective-permute-done
  30.3 3.1 %collective-permute-start.4 = (f32[3,4,16,256]{3,2,1,0:T(8,128)S(1)}, f32[3,4,16,256]{3,2,1,0:T(8,128)S(1)}, u32[]{:S(2)}, u32[]{:S(2)}) collective-permute-start(f32[3,4,16,256]{3,2,1,0:T(8,128)S(1)} %pad_maximum_fusion), channel_id=1, source_target_pairs={{0,7},{1,0},{2,1},{3,2},{4,3},{5,4},{6,5},{7,6},{8,15},{9,8},{10,9... | collective-permute-start | bytes 589832 | tf_op jit(solution)/shard_map/ppermute | solution.py:450
  33.5 2.7 %collective-permute-start.3 = (f32[3,4,16,256]{3,2,1,0:T(8,128)S(1)}, f32[3,4,16,256]{3,2,1,0:T(8,128)S(1)}, u32[]{:S(2)}, u32[]{:S(2)}) collective-permute-start(f32[3,4,16,256]{3,2,1,0:T(8,128)S(1)} %pad_maximum_fusion), channel_id=1, source_target_pairs={{0,1},{1,2},{2,3},{3,4},{4,5},{5,6},{6,7},{7,0},{8,9},{9,10},{10,1... | collective-permute-start | bytes 589832 | tf_op jit(solution)/shard_map/ppermute | solution.py:449
  36.2 4.8 %shard_map.50 = (f32[4480,128]{1,0:T(8,128)S(1)}, f32[4480,128]{1,0:T(8,128)S(1)}) custom-call(s32[3072]{0:T(1024)S(1)} %bitcast.18, s32[2]{0:T(128)S(1)} %pad_add_fusion.refs_1_, f32[1,4,16,256]{3,2,1,0:T(8,128)S(1)} %get-tuple-element.36.refs_2_, f32[1,4,16,256]{3,2,1,0:T(8,128)S(1)} %get-tuple-element.35.refs_3_, ...), custom_call_target="tpu_custom_call", output_to_operand_aliasing={{0}: (5, {}), {1}: (6, {})} | custom-call | tf_op jit(solution)/shard_map/pallas_call | solution.py:391
  41.0 0.0 collective-permute-done.4.refs_3_
  41.0 0.0 collective-permute-done.3.refs_2_
  41.0 10.6 %shard_map.51 = (f32[1,16,1,256]{3,2,1,0:T(1,128)}, f32[4480,128]{1,0:T(8,128)S(1)}, f32[4480,128]{1,0:T(8,128)S(1)}) custom-call(s32[3072]{0:T(1024)S(1)} %bitcast.19, s32[2]{0:T(128)S(1)} %pad_add_fusion.refs_1_, f32[3,4,16,256]{3,2,1,0:T(8,128)S(1)} %collective-permute-done.3.refs_2_, ...), custom_call_target="tpu_custom_call", output_to_operand_aliasing={{1}: (6, {}), {2}: (7, {})} | custom-call | tf_op jit(solution)/shard_map/pallas_call | solution.py:391
  (4 shorter events, 0.1 us)
Async XLA Ops:
  1.6 28.7 %collective-permute-start.2 = (f32[4,16,256]{2,1,0:T(8,128)S(1)}, f32[4,16,256]{2,1,0:T(8,128)S(1)}, u32[]{:S(2)}, u32[]{:S(2)}) collective-permute-start(f32[4,16,256]{2,1,0:T(8,128)S(1)} %get-tuple-element.38.data), channel_id=1, source_target_pairs={{8,0},{16,8},{24,16},{32,24},{40,32},{48,40},{56,48},{64,56},{72,6... | collective-permute-start | bytes 196616 | tf_op jit(solution)/shard_map/ppermute | solution.py:441
  2.9 27.4 %collective-permute-start.1 = (f32[4,16,256]{2,1,0:T(8,128)S(1)}, f32[4,16,256]{2,1,0:T(8,128)S(1)}, u32[]{:S(2)}, u32[]{:S(2)}) collective-permute-start(f32[4,16,256]{2,1,0:T(8,128)S(1)} %get-tuple-element.38.data), channel_id=1, source_target_pairs={{0,8},{8,16},{16,24},{24,32},{32,40},{40,48},{48,56},{56,64},{64,7... | collective-permute-start | bytes 196616 | tf_op jit(solution)/shard_map/ppermute | solution.py:440
  7.5 22.8 %collective-permute-start = (f32[4,16,256]{2,1,0:T(8,128)S(1)}, f32[4,16,256]{2,1,0:T(8,128)S(1)}, u32[]{:S(2)}, u32[]{:S(2)}) collective-permute-start(f32[4,16,256]{2,1,0:T(8,128)S(1)} %get-tuple-element.38.data), channel_id=1, source_target_pairs={{248,256},{504,0},{256,248},{0,504},{249,257},{505,1},{257,249},{1... | collective-permute-start | bytes 196616 | tf_op jit(solution)/shard_map/ppermute | solution.py:439
  30.3 10.6 %collective-permute-start.4 = (f32[3,4,16,256]{3,2,1,0:T(8,128)S(1)}, f32[3,4,16,256]{3,2,1,0:T(8,128)S(1)}, u32[]{:S(2)}, u32[]{:S(2)}) collective-permute-start(f32[3,4,16,256]{3,2,1,0:T(8,128)S(1)} %pad_maximum_fusion), channel_id=1, source_target_pairs={{0,7},{1,0},{2,1},{3,2},{4,3},{5,4},{6,5},{7,6},{8,15},{9,8},{10,9... | collective-permute-start | bytes 589832 | tf_op jit(solution)/shard_map/ppermute | solution.py:450
  33.5 7.5 %collective-permute-start.3 = (f32[3,4,16,256]{3,2,1,0:T(8,128)S(1)}, f32[3,4,16,256]{3,2,1,0:T(8,128)S(1)}, u32[]{:S(2)}, u32[]{:S(2)}) collective-permute-start(f32[3,4,16,256]{3,2,1,0:T(8,128)S(1)} %pad_maximum_fusion), channel_id=1, source_target_pairs={{0,1},{1,2},{2,3},{3,4},{4,5},{5,6},{6,7},{7,0},{8,9},{9,10},{10,1... | collective-permute-start | bytes 589832 | tf_op jit(solution)/shard_map/ppermute | solution.py:449

commit v7 on v6

--- a/solution.py
+++ b/solution.py
@@ -337,15 +337,26 @@
 HBM_SPEC = pl.BlockSpec(memory_space=pl.ANY)
 
 
-def prepare(data, interpret=False):
+def gated(kernel, first_row, skip, count):
+    def run(*refs):
+        here = lax.axis_index("shear") == 0
+
+        @pl.when(here if first_row else jnp.logical_not(here))
+        def _():
+            kernel(*refs[:skip], *refs[skip + count :])
+
+    return run
+
+
+def prepare(data, old=()):
     return pl.pallas_call(
-        prep_kernel,
+        gated(prep_kernel, not old, 1, len(old)),
         out_shape=(
             jax.ShapeDtypeStruct((ROWS, KD), BF16),
             jax.ShapeDtypeStruct((NX, PS), F32),
             jax.ShapeDtypeStruct((24, 128), jnp.int32),
         ),
-        in_specs=[VMEM_SPEC],
+        in_specs=[VMEM_SPEC] * (1 + len(old)),
         out_specs=[VMEM_SPEC] * 3,
         scratch_shapes=[
             pltpu.VMEM((16 * STRIDE, 128), F32),
@@ -356,10 +367,10 @@
             pltpu.SMEM((24, 128), jnp.int32),
             pltpu.SemaphoreType.DMA,
         ],
-        compiler_params=pltpu.CompilerParams(vmem_limit_bytes=40 << 20),
-        interpret=interpret,
-        name="prepare",
-    )(data)
+        input_output_aliases={1 + i: i for i in range(len(old))},
+        compiler_params=pltpu.CompilerParams(vmem_limit_bytes=16 << 20),
+        name="prepare_rest" if old else "prepare_first",
+    )(data, *old)
 
 
 def pair_sums(pencils, fields, group, role, table, shift, inputs, targets, rest, interpret=False):
@@ -387,15 +398,18 @@
         pltpu.SemaphoreType.DMA,
         pltpu.SemaphoreType.DMA,
     ]
-    aliases = {} if role == "first" else {first_in: first_out, first_in + 1: first_out + 1}
+    kernel = functools.partial(pair_kernel, pencils, fields, group, len(inputs), role)
+    if role == "first":
+        kernel = gated(kernel, not rest, first_in, len(rest))
+    aliases = {} if not rest else {first_in: first_out, first_in + 1: first_out + 1}
     return pl.pallas_call(
-        functools.partial(pair_kernel, pencils, fields, group, len(inputs), role),
+        kernel,
         out_shape=out_shape,
         in_specs=[VMEM_SPEC] * (len(inputs) + 3 + len(rest)),
         out_specs=out_specs,
         scratch_shapes=scratch,
         input_output_aliases=aliases,
-        compiler_params=pltpu.CompilerParams(vmem_limit_bytes=40 << 20),
+        compiler_params=pltpu.CompilerParams(vmem_limit_bytes=20 << 20),
         interpret=interpret,
     )(table, shift, *inputs, targets, *rest)
 
@@ -405,8 +419,8 @@
 FAR = ((0, 0, 0, -1), (1, 0, 0, 1), (0, 1, -1, -1), (1, 1, -1, 1), (0, 2, 1, -1), (1, 2, 1, 1))
 
 
-def own_sums(table, shift, data, targets):
-    return pair_sums(OWN, (1,), 16, "first", table, shift, [data[None]], targets, [])
+def own_sums(table, shift, data, targets, old=()):
+    return pair_sums(OWN, (1,), 16, "first", table, shift, [data[None]], targets, old)
 
 
 def side_sums(table, shift, below, above, targets, sums):
@@ -434,16 +448,18 @@
     ]).astype(jnp.int32)
     n_rows = lax.axis_size("shear")
     half = n_rows // 2
-    ends = [(i, (i + 1) % n_rows) for i in (half - 1, n_rows - 1)]
-    inner = [(i, i + 1) for i in range(n_rows) if (i, (i + 1) % n_rows) not in ends]
-    distant = lax.ppermute(data, "shear", ends + [(j, i) for i, j in ends])
+    inner = [(i, (i + 1) % n_rows) for i in range(n_rows) if i != half - 1]
+    middle = lax.ppermute(data, "shear", [(half - 1, half), (half, half - 1)])
     below = lax.ppermute(data, "shear", inner)
+    first = prepare(data)
+    first_sums = own_sums(first[2].reshape(-1), shift, data, first[0])
+    data, first, first_sums = lax.optimization_barrier((data, tuple(first), tuple(first_sums)))
     above = lax.ppermute(data, "shear", [(j, i) for i, j in inner])
-    targets, rank, table = prepare(data)
+    targets, rank, table = prepare(data, first)
     table = table.reshape(-1)
-    sums = own_sums(table, shift, data, targets)
-    below = jnp.where(lax.rem(index, half) == 0, distant, below)
-    above = jnp.where(lax.rem(index, half) == half - 1, distant, above)
+    sums = own_sums(table, shift, data, targets, first_sums)
+    below = jnp.where(index == half, middle, below)
+    above = jnp.where(index == half - 1, middle, above)
     rows = jnp.stack([data, below, above])
     rows, targets, rank, table, shift, sums = lax.optimization_barrier((rows, targets, rank, table, shift, sums))
     low = lax.ppermute(rows, "cross", ring("cross", 1))

time: 51.9 us -> 57 us (1.098)
  the two profiles are of different devices: /device:TPU:1 before, /device:TPU:2 now
where the time goes in v7:
time: 57 us; the launch traced here: 56.6 us
  starting transfers between devices  23.6 us (41%)
  Pallas kernels  23 us (40%)
  local copies, waits for them, and re-layouts  4.69 us (8%)
  other arithmetic  2.44 us (4%)
  waiting for transfers between devices  2.03 us (4%)
  between operations  0.81 us (1%)
    pallas_call x4, Pallas kernels, pair_sums(): pl.pallas_call(kernel, out_shape=out_shape, in_specs=[VMEM_SPEC] * (len(i...  20.1 us
    ppermute x1, starting transfers between devices, shards(): above = lax.ppermute(data, 'shear', [(j, i) for i, j in inner])  13.8 us
    unnamed x7, local copies, waits for them, and re-layouts  4.68 us
    ppermute x1, starting transfers between devices, shards(): below = lax.ppermute(data, 'shear', inner)  3.39 us
    ppermute x1, starting transfers between devices, shards(): high = lax.ppermute(rows, 'cross', ring('cross', -1))  3.14 us
    pallas_call x2, Pallas kernels, prepare(): pl.pallas_call(gated(prep_kernel, not old, 1, len(old)), out_shape=(jax.S...  2.92 us
    ppermute x1, waiting for transfers between devices, shards(): low = lax.ppermute(rows, 'cross', ring('cross', 1))  2.02 us
    ppermute x1, starting transfers between devices, shards(): low = lax.ppermute(rows, 'cross', ring('cross', 1))  1.92 us
  transfers between devices with their start and end apart: 5, of which 1 were waited for; matrix products, arithmetic and copies ran while one was open for 0% of the time, Pallas kernels for 22%

profile of v7, /device:TPU:2, one launch (start us, length us, event | category | flops | bytes accessed | tf_op | source)
XLA Modules:
  0.0 56.6 jit_solution(13323718631999300496)
XLA Ops:
  0.0 0.8 %copy.15 = f32[3,1,16,1,256]{4,2,0,3,1:T(8,128)S(1)} copy(f32[3,1,16,1,256]{4,3,2,1,0:T(1,128)} %param.4) | data formatting | bytes 98304 | tf_op args[0]
  0.8 0.8 %fusion.2 = f32[1,1,16,1,256]{4,2,0,3,1:T(8,128)S(1)} fusion(f32[1,16,1,256]{3,2,1,0:T(1,128)} %param.5, s32[16]{0:T(128)} %bitcast.25), kind=kLoop, calls=%fused_computation.7 | loop fusion | flops 8192 | bytes 32832 | tf_op jit(solution)/shard_map/broadcast_in_dim | solution.py:442
  1.6 0.6 %fusion = (f32[1,4,16,256]{3,2,1,0:T(8,128)}, f32[4,16,256]{2,1,0:T(8,128)S(1)}) fusion(f32[1,1,16,1,256]{4,2,0,3,1:T(8,128)S(1)} %fusion.2, f32[3,1,16,1,256]{4,2,0,3,1:T(8,128)S(1)} %copy.15), kind=kLoop, calls=%fused_computation.4 | loop fusion | flops 16384 | bytes 196608 | tf_op jit(solution)/shard_map/broadcast_in_dim;reshape | solution.py:423
  2.2 3.4 %collective-permute-start.1 = (f32[4,16,256]{2,1,0:T(8,128)S(1)}, f32[4,16,256]{2,1,0:T(8,128)}, u32[]{:S(2)}, u32[]{:S(2)}) collective-permute-start(f32[4,16,256]{2,1,0:T(8,128)S(1)} %get-tuple-element.36.refs_0_), channel_id=1, source_target_pairs={{0,8},{8,16},{16,24},{24,32},{32,40},{40,48},{48,56},{56,64},{64,7... | collective-permute-start | bytes 196616 | tf_op jit(solution)/shard_map/ppermute | solution.py:453
  5.6 1.3 %collective-permute-start = (f32[4,16,256]{2,1,0:T(8,128)S(1)}, f32[4,16,256]{2,1,0:T(8,128)}, u32[]{:S(2)}, u32[]{:S(2)}) collective-permute-start(f32[4,16,256]{2,1,0:T(8,128)S(1)} %get-tuple-element.36.refs_0_), channel_id=1, source_target_pairs={{248,256},{256,248},{249,257},{257,249},{250,258},{258,250},{251,2... | collective-permute-start | bytes 196616 | tf_op jit(solution)/shard_map/ppermute | solution.py:452
  7.6 0.1 pad_add_fusion.refs_1_
  7.7 0.0 copy-start.2
  7.7 0.8 %copy-done.2 = f32[1,4,16,256]{3,2,1,0:T(8,128)S(1)} copy-done((f32[1,4,16,256]{3,2,1,0:T(8,128)S(1)}, f32[1,4,16,256]{3,2,1,0:T(8,128)}, u32[]{:S(2)}) %copy-start.2) | copy-done | bytes 65560
  8.5 0.0 copy-start
  8.5 1.4 %copy-done = f32[4480,128]{1,0:T(8,128)} copy-done((f32[4480,128]{1,0:T(8,128)}, f32[4480,128]{1,0:T(8,128)S(1)}, u32[]{:S(2)}) %copy-start) | copy-done | bytes 2293784
  9.9 13.8 %collective-permute-start.2 = (f32[4,16,256]{2,1,0:T(8,128)S(1)}, f32[4,16,256]{2,1,0:T(8,128)}, u32[]{:S(2)}, u32[]{:S(2)}) collective-permute-start(f32[4,16,256]{2,1,0:T(8,128)S(1)} %get-tuple-element.36.refs_0_), channel_id=1, source_target_pairs={{8,0},{16,8},{24,16},{32,24},{40,32},{48,40},{56,48},{64,56},{72,6... | collective-permute-start | bytes 196616 | tf_op jit(solution)/shard_map/ppermute | solution.py:457
  23.8 2.9 %prepare_rest.1 = (bf16[4480,32]{1,0:T(8,128)(2,1)S(1)}, f32[16,256]{1,0:T(8,128)S(1)}, s32[24,128]{1,0:T(8,128)S(1)}) custom-call(f32[4,16,256]{2,1,0:T(8,128)S(1)} %get-tuple-element.36.refs_0_, bf16[4480,32]{1,0:T(8,128)(2,1)S(1)} %get-tuple-element.37.refs_3_.refs_1_, ...), custom_call_target="tpu_custom_call", output_to_operand_aliasing={{0}: (1, {}), {1}: (2, {}), {2}: (3, {})} | custom-call | tf_op jit(solution)/shard_map/prepare_rest/pallas_call | solution.py:352
  26.7 0.0 copy-start.1
  26.7 1.6 %copy-done.1 = f32[4480,128]{1,0:T(8,128)S(1)} copy-done((f32[4480,128]{1,0:T(8,128)S(1)}, f32[4480,128]{1,0:T(8,128)}, u32[]{:S(2)}) %copy-start.1) | copy-done | bytes 2293784
  28.4 4.7 %shard_map.50 = (f32[4480,128]{1,0:T(8,128)S(1)}, f32[4480,128]{1,0:T(8,128)S(1)}) custom-call(s32[3072]{0:T(1024)S(1)} %bitcast.22, s32[2]{0:T(128)S(1)} %pad_add_fusion.refs_1_, f32[1,4,16,256]{3,2,1,0:T(8,128)S(1)} %bitcast.19, bf16[4480,32]{1,0:T(8,128)(2,1)S(1)} %get-tuple-element.50.refs_3_.refs_4_, ...), custom_call_target="tpu_custom_call", output_to_operand_aliasing={{0}: (4, {}), {1}: (5, {})} | custom-call | tf_op jit(solution)/shard_map/pallas_call | solution.py:405
  33.0 0.0 collective-permute-done.1
  33.1 0.0 collective-permute-done
  33.1 0.0 collective-permute-done.2
  33.1 0.9 %select_bitcast_fusion.1 = (f32[1,4,16,256]{3,2,1,0:T(8,128)S(1)}, f32[1,4,16,256]{3,2,1,0:T(8,128)S(1)}) fusion(f32[4,16,256]{2,1,0:T(8,128)} %collective-permute-done, f32[4,16,256]{2,1,0:T(8,128)} %collective-permute-done.1, pred[]{:T(512)S(6)} %eq.14, f32[4,16,256]{2,1,0:T(8,128)} %collective-permute-done.2, pred[]{:T(512)S(6)} %eq.15), kind=kLoop, calls=%fused_computation.3 | loop fusion | flops 32768 | bytes 327682 | tf_op jit(solution)/shard_map/stack | solution.py:463
  34.0 3.1 %collective-permute-start.4 = (f32[3,4,16,256]{3,2,1,0:T(8,128)S(1)}, f32[3,4,16,256]{3,2,1,0:T(8,128)S(1)}, u32[]{:S(2)}, u32[]{:S(2)}) collective-permute-start(f32[3,4,16,256]{3,2,1,0:T(8,128)S(1)} %pad_maximum_fusion), channel_id=1, source_target_pairs={{0,7},{1,0},{2,1},{3,2},{4,3},{5,4},{6,5},{7,6},{8,15},{9,8},{10,9... | collective-permute-start | bytes 589832 | tf_op jit(solution)/shard_map/ppermute | solution.py:466
  37.2 1.9 %collective-permute-start.3 = (f32[3,4,16,256]{3,2,1,0:T(8,128)S(1)}, f32[3,4,16,256]{3,2,1,0:T(8,128)S(1)}, u32[]{:S(2)}, u32[]{:S(2)}) collective-permute-start(f32[3,4,16,256]{3,2,1,0:T(8,128)S(1)} %pad_maximum_fusion), channel_id=1, source_target_pairs={{0,1},{1,2},{2,3},{3,4},{4,5},{5,6},{6,7},{7,0},{8,9},{9,10},{10,1... | collective-permute-start | bytes 589832 | tf_op jit(solution)/shard_map/ppermute | solution.py:465
  39.1 4.8 %shard_map.51 = (f32[4480,128]{1,0:T(8,128)S(1)}, f32[4480,128]{1,0:T(8,128)S(1)}) custom-call(s32[3072]{0:T(1024)S(1)} %bitcast.23, s32[2]{0:T(128)S(1)} %pad_add_fusion.refs_1_, f32[1,4,16,256]{3,2,1,0:T(8,128)S(1)} %get-tuple-element.58.refs_2_, f32[1,4,16,256]{3,2,1,0:T(8,128)S(1)} %get-tuple-element.57.refs_3_, ...), custom_call_target="tpu_custom_call", output_to_operand_aliasing={{0}: (5, {}), {1}: (6, {})} | custom-call | tf_op jit(solution)/shard_map/pallas_call | solution.py:405
  43.9 0.0 collective-permute-done.4.refs_3_
  44.0 2.0 %collective-permute-done.3.refs_2_ = f32[3,4,16,256]{3,2,1,0:T(8,128)S(1)} collective-permute-done((f32[3,4,16,256]{3,2,1,0:T(8,128)S(1)}, f32[3,4,16,256]{3,2,1,0:T(8,128)S(1)}, u32[]{:S(2)}, u32[]{:S(2)}) %collective-permute-start.3) | collective-permute-done | bytes 196640 | tf_op jit(solution)/shard_map/ppermute | solution.py:465
  46.0 10.6 %shard_map.52 = (f32[1,16,1,256]{3,2,1,0:T(1,128)}, f32[4480,128]{1,0:T(8,128)S(1)}, f32[4480,128]{1,0:T(8,128)S(1)}) custom-call(s32[3072]{0:T(1024)S(1)} %bitcast.24, s32[2]{0:T(128)S(1)} %pad_add_fusion.refs_1_, f32[3,4,16,256]{3,2,1,0:T(8,128)S(1)} %collective-permute-done.3.refs_2_, ...), custom_call_target="tpu_custom_call", output_to_operand_aliasing={{1}: (6, {}), {2}: (7, {})} | custom-call | tf_op jit(solution)/shard_map/pallas_call | solution.py:405
  (4 shorter events, 0.1 us)
Async XLA Ops:
  2.2 30.8 %collective-permute-start.1 = (f32[4,16,256]{2,1,0:T(8,128)S(1)}, f32[4,16,256]{2,1,0:T(8,128)}, u32[]{:S(2)}, u32[]{:S(2)}) collective-permute-start(f32[4,16,256]{2,1,0:T(8,128)S(1)} %get-tuple-element.36.refs_0_), channel_id=1, source_target_pairs={{0,8},{8,16},{16,24},{24,32},{32,40},{40,48},{48,56},{56,64},{64,7... | collective-permute-start | bytes 196616 | tf_op jit(solution)/shard_map/ppermute | solution.py:453
  5.6 27.4 %collective-permute-start = (f32[4,16,256]{2,1,0:T(8,128)S(1)}, f32[4,16,256]{2,1,0:T(8,128)}, u32[]{:S(2)}, u32[]{:S(2)}) collective-permute-start(f32[4,16,256]{2,1,0:T(8,128)S(1)} %get-tuple-element.36.refs_0_), channel_id=1, source_target_pairs={{248,256},{256,248},{249,257},{257,249},{250,258},{258,250},{251,2... | collective-permute-start | bytes 196616 | tf_op jit(solution)/shard_map/ppermute | solution.py:452
  7.7 0.8 %copy-start.2 = (f32[1,4,16,256]{3,2,1,0:T(8,128)S(1)}, f32[1,4,16,256]{3,2,1,0:T(8,128)}, u32[]{:S(2)}) copy-start(f32[1,4,16,256]{3,2,1,0:T(8,128)} %get-tuple-element.61.refs_2_) | copy-start | bytes 196612
  8.5 1.4 %copy-start = (f32[4480,128]{1,0:T(8,128)}, f32[4480,128]{1,0:T(8,128)S(1)}, u32[]{:S(2)}) copy-start(f32[4480,128]{1,0:T(8,128)S(1)} %get-tuple-element.44.refs_5_) | copy-start | bytes 6881284
  9.9 23.1 %collective-permute-start.2 = (f32[4,16,256]{2,1,0:T(8,128)S(1)}, f32[4,16,256]{2,1,0:T(8,128)}, u32[]{:S(2)}, u32[]{:S(2)}) collective-permute-start(f32[4,16,256]{2,1,0:T(8,128)S(1)} %get-tuple-element.36.refs_0_), channel_id=1, source_target_pairs={{8,0},{16,8},{24,16},{32,24},{40,32},{48,40},{56,48},{64,56},{72,6... | collective-permute-start | bytes 196616 | tf_op jit(solution)/shard_map/ppermute | solution.py:457
  26.7 1.6 %copy-start.1 = (f32[4480,128]{1,0:T(8,128)S(1)}, f32[4480,128]{1,0:T(8,128)}, u32[]{:S(2)}) copy-start(f32[4480,128]{1,0:T(8,128)} %copy-done) | copy-start | bytes 6881284
  34.0 9.9 %collective-permute-start.4 = (f32[3,4,16,256]{3,2,1,0:T(8,128)S(1)}, f32[3,4,16,256]{3,2,1,0:T(8,128)S(1)}, u32[]{:S(2)}, u32[]{:S(2)}) collective-permute-start(f32[3,4,16,256]{3,2,1,0:T(8,128)S(1)} %pad_maximum_fusion), channel_id=1, source_target_pairs={{0,7},{1,0},{2,1},{3,2},{4,3},{5,4},{6,5},{7,6},{8,15},{9,8},{10,9... | collective-permute-start | bytes 589832 | tf_op jit(solution)/shard_map/ppermute | solution.py:466
  37.2 8.8 %collective-permute-start.3 = (f32[3,4,16,256]{3,2,1,0:T(8,128)S(1)}, f32[3,4,16,256]{3,2,1,0:T(8,128)S(1)}, u32[]{:S(2)}, u32[]{:S(2)}) collective-permute-start(f32[3,4,16,256]{3,2,1,0:T(8,128)S(1)} %pad_maximum_fusion), channel_id=1, source_target_pairs={{0,1},{1,2},{2,3},{3,4},{4,5},{5,6},{6,7},{7,0},{8,9},{9,10},{10,1... | collective-permute-start | bytes 589832 | tf_op jit(solution)/shard_map/ppermute | solution.py:465

commit v8 on v5

--- a/solution.py
+++ b/solution.py
@@ -6,6 +6,7 @@
 from jax.experimental import pallas as pl
 from jax.experimental.pallas import tpu as pltpu
 from jax.sharding import PartitionSpec as P
+
 
 NX = 16
 PS = 256
@@ -361,7 +362,7 @@
     )(data)
 
 
-def pair_sums(pencils, fields, group, role, table, shift, inputs, targets, rest, name, interpret=False):
+def pair_sums(pencils, fields, group, role, table, shift, inputs, targets, rest, interpret=False):
     n = len(pencils)
     out_shape = [jax.ShapeDtypeStruct((ROWS, 128), F32)] * 2
     out_specs = [VMEM_SPEC] * 2
@@ -371,8 +372,8 @@
         pltpu.VMEM((n, RC * STRIDE, 128), F32),
         pltpu.VMEM((n, RC * STRIDE, 128), F32),
         pltpu.VMEM((n * RC, KD, PS), BF16),
-        pltpu.VMEM((n * RC, 128), F32),
-        pltpu.VMEM((n * RC, 128), F32),
+        pltpu.VMEM((n * RC + 8, 128), F32),
+        pltpu.VMEM((n * RC + 8, 128), F32),
         pltpu.VMEM((group, BLOCK, PS * len(fields)), F32),
     ]
     if role == "last":
@@ -396,7 +397,6 @@
         input_output_aliases=aliases,
         compiler_params=pltpu.CompilerParams(vmem_limit_bytes=40 << 20),
         interpret=interpret,
-        name=name,
     )(table, shift, *inputs, targets, *rest)
 
 
@@ -406,15 +406,15 @@
 
 
 def own_sums(table, shift, data, targets):
-    return pair_sums(OWN, (1,), 16, "first", table, shift, [data[None]], targets, [], "own")
+    return pair_sums(OWN, (1,), 16, "first", table, shift, [data[None]], targets, [])
 
 
 def side_sums(table, shift, below, above, targets, sums):
-    return pair_sums(SIDE, (2,), 16, "next", table, shift, [below[None], above[None]], targets, sums, "side")
+    return pair_sums(SIDE, (2,), 16, "next", table, shift, [below[None], above[None]], targets, sums)
 
 
 def far_sums(table, shift, low, high, targets, rank, sums):
-    return pair_sums(FAR, (3, 4), 8, "last", table, shift, [low, high], targets, [rank, *sums], "far")[0]
+    return pair_sums(FAR, (3, 4), 8, "last", table, shift, [low, high], targets, [rank, *sums])[0]
 
 
 def ring(axis, distance):

time: 56.2 us -> 54.4 us (0.968); the launches traced: 56.8 us -> 54.1 us
  Pallas kernels: 26.6 us -> 22.9 us
  waiting for transfers between devices: 2.69 us -> 3.6 us
    pallas_call x3, Pallas kernels: 23.7 us -> 20.1 us  [pair_sums(): pl.pallas_call(functools.partial(pair_kernel, pencils, fields, group, len...]
    ppermute x1, waiting for transfers between devices: 2.68 us -> 3.59 us  [shards(): below = lax.ppermute(data, 'shear', ring('shear', 1))]
  transfers between devices with their start and end apart: 4 -> 4, of which waited for: 1 -> 1; matrix products, arithmetic and copies ran while one was open for 0% -> 0% of each run, Pallas kernels for 25% -> 23%
where the time goes in v8:
time: 54.4 us; the launch traced here: 54.1 us
  starting transfers between devices  25.1 us (46%)
  Pallas kernels  22.9 us (42%)
  waiting for transfers between devices  3.6 us (7%)
  other arithmetic  0.89 us (2%)
  local copies, waits for them, and re-layouts  0.81 us (1%)
  between operations  0.76 us (1%)
    pallas_call x3, Pallas kernels, pair_sums(): pl.pallas_call(functools.partial(pair_kernel, pencils, fields, group, len...  20.1 us
    ppermute x1, starting transfers between devices, shards(): above = lax.ppermute(data, 'shear', ring('shear', -1))  16.6 us
    ppermute x1, starting transfers between devices, shards(): high = lax.ppermute(rows, 'cross', ring('cross', -1))  3.98 us
    ppermute x1, waiting for transfers between devices, shards(): below = lax.ppermute(data, 'shear', ring('shear', 1))  3.59 us
    pallas_call x1, Pallas kernels, prepare(): pl.pallas_call(prep_kernel, out_shape=(jax.ShapeDtypeStruct((ROWS, KD), B...  2.88 us
    ppermute x1, starting transfers between devices, shards(): low = lax.ppermute(rows, 'cross', ring('cross', 1))  2.62 us
    ppermute x1, starting transfers between devices, shards(): below = lax.ppermute(data, 'shear', ring('shear', 1))  1.92 us
  transfers between devices with their start and end apart: 4, of which 1 were waited for; matrix products, arithmetic and copies ran while one was open for 0% of the time, Pallas kernels for 23%

profile of v8, /device:TPU:1, one launch (start us, length us, event | category | flops | bytes accessed | tf_op | source)
XLA Modules:
  0.0 54.1 jit_solution(13355952852825228802)
XLA Ops:
  0.0 0.8 %copy.10 = f32[3,1,16,1,256]{4,2,0,3,1:T(8,128)S(1)} copy(f32[3,1,16,1,256]{4,3,2,1,0:T(1,128)} %param.4) | data formatting | bytes 98304 | tf_op args[0]
  0.8 0.8 %fusion.2 = f32[1,1,16,1,256]{4,2,0,3,1:T(8,128)S(1)} fusion(f32[1,16,1,256]{3,2,1,0:T(1,128)} %param.5, s32[16]{0:T(128)} %bitcast.20), kind=kLoop, calls=%fused_computation.5 | loop fusion | flops 8192 | bytes 32832 | tf_op jit(solution)/shard_map/broadcast_in_dim | solution.py:428
  1.6 16.6 %collective-permute-start.1 = (f32[4,16,256]{2,1,0:T(8,128)S(1)}, f32[4,16,256]{2,1,0:T(8,128)S(1)}, u32[]{:S(2)}, u32[]{:S(2)}) collective-permute-start(f32[4,16,256]{2,1,0:T(8,128)S(1)} %get-tuple-element.38.data), channel_id=1, source_target_pairs={{0,504},{8,0},{16,8},{24,16},{32,24},{40,32},{48,40},{56,48},{64,5... | collective-permute-start | bytes 196616 | tf_op jit(solution)/shard_map/ppermute | solution.py:436
  18.2 1.9 %collective-permute-start = (f32[4,16,256]{2,1,0:T(8,128)S(1)}, f32[4,16,256]{2,1,0:T(8,128)S(1)}, u32[]{:S(2)}, u32[]{:S(2)}) collective-permute-start(f32[4,16,256]{2,1,0:T(8,128)S(1)} %get-tuple-element.38.data), channel_id=1, source_target_pairs={{0,8},{8,16},{16,24},{24,32},{32,40},{40,48},{48,56},{56,64},{64,7... | collective-permute-start | bytes 196616 | tf_op jit(solution)/shard_map/ppermute | solution.py:435
  20.1 2.9 %prepare.1 = (bf16[4480,32]{1,0:T(8,128)(2,1)S(1)}, f32[16,256]{1,0:T(8,128)S(1)}, s32[24,128]{1,0:T(8,128)S(1)}) custom-call(f32[4,16,256]{2,1,0:T(8,128)S(1)} %get-tuple-element.38.data), custom_call_target="tpu_custom_call" | custom-call | tf_op jit(solution)/shard_map/prepare/pallas_call | solution.py:341
  23.6 0.1 pad_add_fusion.refs_1_
  23.7 4.7 %shard_map.49 = (f32[4480,128]{1,0:T(8,128)S(1)}, f32[4480,128]{1,0:T(8,128)S(1)}) custom-call(s32[3072]{0:T(1024)S(1)} %bitcast.15, s32[2]{0:T(128)S(1)} %pad_add_fusion.refs_1_, f32[1,4,16,256]{3,2,1,0:T(8,128)S(1)} %get-tuple-element.37.refs_2_, bf16[4480,32]{1,0:T(8,128)(2,1)S(1)} %get-tuple-element.28.refs_3_.refs_4_), custom_call_target="tpu_custom_call" | custom-call | tf_op jit(solution)/shard_map/pallas_call | solution.py:391
  28.4 0.0 collective-permute-done.1
  28.4 3.6 %collective-permute-done = f32[4,16,256]{2,1,0:T(8,128)S(1)} collective-permute-done((f32[4,16,256]{2,1,0:T(8,128)S(1)}, f32[4,16,256]{2,1,0:T(8,128)S(1)}, u32[]{:S(2)}, u32[]{:S(2)}) %collective-permute-start) | collective-permute-done | bytes 65568 | tf_op jit(solution)/shard_map/ppermute | solution.py:435
  32.0 4.0 %collective-permute-start.3 = (f32[3,4,16,256]{3,2,1,0:T(8,128)S(1)}, f32[3,4,16,256]{3,2,1,0:T(8,128)S(1)}, u32[]{:S(2)}, u32[]{:S(2)}) collective-permute-start(f32[3,4,16,256]{3,2,1,0:T(8,128)S(1)} %pad_maximum_fusion), channel_id=1, source_target_pairs={{0,7},{1,0},{2,1},{3,2},{4,3},{5,4},{6,5},{7,6},{8,15},{9,8},{10,9... | collective-permute-start | bytes 589832 | tf_op jit(solution)/shard_map/ppermute | solution.py:443
  36.0 2.6 %collective-permute-start.2 = (f32[3,4,16,256]{3,2,1,0:T(8,128)S(1)}, f32[3,4,16,256]{3,2,1,0:T(8,128)S(1)}, u32[]{:S(2)}, u32[]{:S(2)}) collective-permute-start(f32[3,4,16,256]{3,2,1,0:T(8,128)S(1)} %pad_maximum_fusion), channel_id=1, source_target_pairs={{0,1},{1,2},{2,3},{3,4},{4,5},{5,6},{6,7},{7,0},{8,9},{9,10},{10,1... | collective-permute-start | bytes 589832 | tf_op jit(solution)/shard_map/ppermute | solution.py:442
  38.7 4.8 %shard_map.50 = (f32[4480,128]{1,0:T(8,128)S(1)}, f32[4480,128]{1,0:T(8,128)S(1)}) custom-call(s32[3072]{0:T(1024)S(1)} %bitcast.16, s32[2]{0:T(128)S(1)} %pad_add_fusion.refs_1_, f32[1,4,16,256]{3,2,1,0:T(8,128)S(1)} %get-tuple-element.36.refs_2_, f32[1,4,16,256]{3,2,1,0:T(8,128)S(1)} %get-tuple-element.35.refs_3_, ...), custom_call_target="tpu_custom_call", output_to_operand_aliasing={{0}: (5, {}), {1}: (6, {})} | custom-call | tf_op jit(solution)/shard_map/pallas_call | solution.py:391
  43.5 0.0 collective-permute-done.3.refs_3_
  43.5 0.0 collective-permute-done.2.refs_2_
  43.5 10.6 %shard_map.51 = (f32[1,16,1,256]{3,2,1,0:T(1,128)}, f32[4480,128]{1,0:T(8,128)S(1)}, f32[4480,128]{1,0:T(8,128)S(1)}) custom-call(s32[3072]{0:T(1024)S(1)} %bitcast.17, s32[2]{0:T(128)S(1)} %pad_add_fusion.refs_1_, f32[3,4,16,256]{3,2,1,0:T(8,128)S(1)} %collective-permute-done.2.refs_2_, ...), custom_call_target="tpu_custom_call", output_to_operand_aliasing={{1}: (6, {}), {2}: (7, {})} | custom-call | tf_op jit(solution)/shard_map/pallas_call | solution.py:391
  (3 shorter events, 0.0 us)
Async XLA Ops:
  1.6 26.8 %collective-permute-start.1 = (f32[4,16,256]{2,1,0:T(8,128)S(1)}, f32[4,16,256]{2,1,0:T(8,128)S(1)}, u32[]{:S(2)}, u32[]{:S(2)}) collective-permute-start(f32[4,16,256]{2,1,0:T(8,128)S(1)} %get-tuple-element.38.data), channel_id=1, source_target_pairs={{0,504},{8,0},{16,8},{24,16},{32,24},{40,32},{48,40},{56,48},{64,5... | collective-permute-start | bytes 196616 | tf_op jit(solution)/shard_map/ppermute | solution.py:436
  18.2 13.8 %collective-permute-start = (f32[4,16,256]{2,1,0:T(8,128)S(1)}, f32[4,16,256]{2,1,0:T(8,128)S(1)}, u32[]{:S(2)}, u32[]{:S(2)}) collective-permute-start(f32[4,16,256]{2,1,0:T(8,128)S(1)} %get-tuple-element.38.data), channel_id=1, source_target_pairs={{0,8},{8,16},{16,24},{24,32},{32,40},{40,48},{48,56},{56,64},{64,7... | collective-permute-start | bytes 196616 | tf_op jit(solution)/shard_map/ppermute | solution.py:435
  32.0 11.4 %collective-permute-start.3 = (f32[3,4,16,256]{3,2,1,0:T(8,128)S(1)}, f32[3,4,16,256]{3,2,1,0:T(8,128)S(1)}, u32[]{:S(2)}, u32[]{:S(2)}) collective-permute-start(f32[3,4,16,256]{3,2,1,0:T(8,128)S(1)} %pad_maximum_fusion), channel_id=1, source_target_pairs={{0,7},{1,0},{2,1},{3,2},{4,3},{5,4},{6,5},{7,6},{8,15},{9,8},{10,9... | collective-permute-start | bytes 589832 | tf_op jit(solution)/shard_map/ppermute | solution.py:443
  36.0 7.5 %collective-permute-start.2 = (f32[3,4,16,256]{3,2,1,0:T(8,128)S(1)}, f32[3,4,16,256]{3,2,1,0:T(8,128)S(1)}, u32[]{:S(2)}, u32[]{:S(2)}) collective-permute-start(f32[3,4,16,256]{3,2,1,0:T(8,128)S(1)} %pad_maximum_fusion), channel_id=1, source_target_pairs={{0,1},{1,2},{2,3},{3,4},{4,5},{5,6},{6,7},{7,0},{8,9},{9,10},{10,1... | collective-permute-start | bytes 589832 | tf_op jit(solution)/shard_map/ppermute | solution.py:442
